TPU v7x, 32 devices: a whole 2x2x4 slice. The times are simulated.
32 devices in a mesh: dp: 2 (over x), tp: 4 (over z), sp: 4 (over y, core).
Axes of the slice: x: 2, y: 2, z: 4, core: 2. Of those that a mesh axis runs over, the one named last changes fastest.
Arguments:
- hidden: bfloat16 [512, 4096], P('dp'), parts along dimension 0
- lengths: int32 [512], P('dp'), parts along dimension 0
- k_cache: bfloat16 [512, 128, 8, 128], P('dp', 'sp', 'tp'), parts along dimension 0
- v_cache: bfloat16 [512, 128, 8, 128], P('dp', 'sp', 'tp'), parts along dimension 0
- norm_gain: bfloat16 [4096], replicated
- w_query: bfloat16 [4096, 4096], P(None, 'tp')
- w_key: bfloat16 [4096, 1024], P(None, 'tp')
- w_value: bfloat16 [4096, 1024], P(None, 'tp')
- w_out: bfloat16 [4096, 4096], P('tp')
Outputs:
- output 1: bfloat16 [512, 4096], P('dp'), parts along dimension 0
- output 2: bfloat16 [512, 128, 8, 128], P('dp', 'sp', 'tp'), parts along dimension 0
- output 3: bfloat16 [512, 128, 8, 128], P('dp', 'sp', 'tp'), parts along dimension 0
There are 2 independent parts. A program takes and returns all parts, laid end to end along the dimension named above; an argument that names none is the same for every part.
All inputs are finite; a program needn't handle non-finite values.
Results may differ from a plain program's by a relative error of at most 0.00451752.
Values sent between devices are 32-bit elements.
A program may use at most 1 GiB of HBM per device.

v0:
```python
import jax
import jax.numpy as jnp
from jax import lax
from jax.sharding import PartitionSpec as P

EPS = 1e-6
NEG_BIG = -1e30


def solution(mesh):
    cache_spec = P('dp', 'sp', 'tp', None)

    def local_step(hidden, lengths, k_cache, v_cache, norm_gain, w_query, w_key, w_value, w_out):
        batch, seq_block, kv_local, head_dim = k_cache.shape
        heads_local = w_query.shape[1] // head_dim
        group = heads_local // kv_local
        hid_f32 = hidden.astype(jnp.float32)
        inv_rms = lax.rsqrt(jnp.mean(hid_f32 * hid_f32, axis=-1, keepdims=True) + EPS)
        normed = (hid_f32 * inv_rms * norm_gain.astype(jnp.float32)).astype(jnp.bfloat16)
        query = jnp.dot(normed, w_query, preferred_element_type=jnp.float32).astype(jnp.bfloat16)
        query = query.reshape(batch, kv_local, group, head_dim)
        new_key = jnp.dot(normed, w_key, preferred_element_type=jnp.float32).astype(jnp.bfloat16)
        new_value = jnp.dot(normed, w_value, preferred_element_type=jnp.float32).astype(jnp.bfloat16)
        positions = lax.axis_index('sp') * seq_block + jnp.arange(seq_block)
        at_slot = (positions[None, :] == lengths[:, None])[:, :, None, None]
        k_new = jnp.where(at_slot, new_key.reshape(batch, 1, kv_local, head_dim), k_cache)
        v_new = jnp.where(at_slot, new_value.reshape(batch, 1, kv_local, head_dim), v_cache)
        scores = jnp.einsum('bkgd,btkd->bkgt', query, k_new, preferred_element_type=jnp.float32) * (head_dim ** -0.5)
        valid = (positions[None, :] <= lengths[:, None])[:, None, None, :]
        scores = jnp.where(valid, scores, NEG_BIG)
        local_peak = jnp.max(scores, axis=-1, keepdims=True)
        exp_vals = jnp.where(valid, jnp.exp(scores - local_peak), 0.0)
        local_denom = jnp.sum(exp_vals, axis=-1, keepdims=True)
        local_acc = jnp.einsum('bkgt,btkd->bkgd', exp_vals.astype(jnp.bfloat16), v_new, preferred_element_type=jnp.float32)
        global_peak = lax.pmax(local_peak, 'sp')
        rescale = jnp.exp(local_peak - global_peak)
        total_acc, total_denom = lax.psum((local_acc * rescale, local_denom * rescale), 'sp')
        attn_out = (total_acc / total_denom).astype(jnp.bfloat16).reshape(batch, heads_local * head_dim)
        part_out = jnp.dot(attn_out, w_out, preferred_element_type=jnp.float32)
        head_sum = lax.psum(part_out, 'tp')
        hidden_out = (hid_f32 + head_sum).astype(jnp.bfloat16)
        return hidden_out, k_new, v_new

    return jax.shard_map(
        local_step,
        mesh=mesh,
        in_specs=(P('dp', None), P('dp'), cache_spec, cache_spec, P(None), P(None, 'tp'), P(None, 'tp'), P(None, 'tp'), P('tp', None)),
        out_specs=(P('dp', None), cache_spec, cache_spec),
        check_vma=False,
    )
```

profile of v0, /device:TPU:0, one launch (start us, length us, event | category | flops | bytes accessed | tf_op | source)
XLA Modules:
  0.0 281.2 jit_solution(12331212477215118053)
XLA Ops:
  7.2 0.0 copy-start
  7.2 0.0 all-reduce.3.cloned.1.call-start
  7.2 2.2 fusion
  9.5 0.7 convert_element_type.28
  10.2 0.0 copy-done
  10.2 2.7 convolution_convert_fusion.2
  12.9 0.1 copy.12
  13.0 3.4 %convolution_convert_fusion.1 = bf16[256,256]{0,1:T(8,128)(2,1)S(1)} fusion(bf16[4096,256]{1,0:T(8,128)(2,1)} %param.16, bf16[256,4096]{1,0:T(8,128)(2,1)} %param.9, f32[4096]{0:T(1024)S(1)} %convert_element_type.28, f32[256]{0:T(256)S(1)} %add_rsqrt_fusion), kind=kOutput, calls=%fused_computation.17 | convolution fusion | flops 541130752 | bytes 4342784 | tf_op jit(solution)/shard_map/dot_general | solution.py:23
  16.4 0.1 copy.14
  16.5 0.0 copy-start.2
  16.6 6.4 %convolution_convert_fusion = bf16[256,1024]{1,0:T(8,128)(2,1)S(1)} fusion(bf16[4096,1024]{1,0:T(8,128)(2,1)} %param.14, bf16[256,4096]{1,0:T(8,128)(2,1)} %param.9, f32[4096]{0:T(1024)S(1)} %convert_element_type.28, f32[256]{0:T(256)S(1)} %add_rsqrt_fusion), kind=kOutput, calls=%fused_computation.15 | convolution fusion | flops 2151940096 | bytes 11027456 | tf_op jit(solution)/shard_map/dot_general | solution.py:20
  23.0 0.4 reshape.79
  23.3 0.0 copy-done.2
  23.4 0.1 broadcast_compare_fusion.1
  23.5 13.8 %broadcast_select_fusion.1 = (bf16[256,32,2,128]{3,2,1,0:T(2,128)(2,1)S(1)}, bf16[256,32,2,128]{3,2,1,0:T(2,128)(2,1)}) fusion(bf16[256,32,2,128]{3,2,1,0:T(2,128)(2,1)} %param.11, pred[256,32]{1,0:T(8,128)(4,1)S(1)} %get-tuple-element.8, bf16[256,2,128]{2,1,0:T(2,128)(2,1)S(1)} %copy.12, bf16[256,32,2,128]{3,2,1,0:T(2,128)(2,1)} %param.12, ...), kind=kLoop, calls=%fused_computation.1 | loop fusion | flops 4194304 | bytes 17047552 | tf_op jit(solution)/shard_map/jit(_where)/select_n | solution.py:26
  37.3 0.0 copy-start.1
  37.3 2.0 copy-done.1
  39.3 3.4 %fusion.29 = (f32[256,2,4]{2,1,0:T(2,128)S(1)}, f32[256,2,4,32]{3,2,1,0:T(4,128)}) fusion(bf16[256,2,4,128]{3,2,1,0:T(4,128)(2,1)S(1)} %reshape.79, bf16[256,32,2,128]{3,2,1,0:T(2,128)(2,1)S(1)} %get-tuple-element.5, pred[256,32]{1,0:T(8,128)(4,1)S(1)} %get-tuple-element.7), kind=kOutput, calls=%fused_computation.35 | convolution fusion | flops 16971776 | bytes 4997120 | tf_op jit(solution)/shard_map/bkgd,btkd->bkgt/dot_general | solution.py:28
  42.7 16.2 %pmax.7 = f32[256,2,4,1]{2,1,0,3:T(2,128)S(1)} all-reduce(f32[256,2,4,1]{2,1,0,3:T(2,128)S(1)} %bitcast.19), channel_id=1, replica_groups=mesh['dp'=2,'tp'=4,'sp'=4] {'sp'}, use_global_device_ids=true, to_apply=%region_2.3 | all-reduce | flops 2048 | bytes 16384 | tf_op jit(solution)/shard_map/pmax | solution.py:35
  58.9 2.5 fusion.17
  61.4 0.3 fusion.23
  61.6 4.9 %fusion.11 = f32[256,2,4,128]{3,2,1,0:T(4,128)} fusion(bf16[256,32,2,128]{3,2,1,0:T(2,128)(2,1)} %get-tuple-element.6, f32[256,2,4,32]{3,2,1,0:T(4,128)} %get-tuple-element.10, f32[256,2,4]{2,1,0:T(2,128)S(1)} %get-tuple-element.4, f32[256,2,4]{2,1,0:T(2,128)S(1)} %get-tuple-element.9, pred[256,32]{1,0:T(8,128)(4,1)S(1)} %get-tuple-element.7), kind=kOutput, calls=%fused_computation.14 | convolution fusion | flops 17235968 | bytes 5529600 | tf_op jit(solution)/shard_map/bkgt,btkd->bkgd/dot_general | solution.py:34
  66.5 0.0 all-reduce.3.cloned.1.call-update
  66.5 0.0 all-reduce.5.cloned.1.call-start
  66.6 15.0 %psum.22 = f32[256,2,4]{2,1,0:T(2,128)S(1)} all-reduce(f32[256,2,4]{2,1,0:T(2,128)S(1)} %get-tuple-element.3), channel_id=1, replica_groups=mesh['dp'=2,'tp'=4,'sp'=4] {'sp'}, use_global_device_ids=true, to_apply=%region_5.6 | all-reduce | flops 2048 | bytes 16384 | tf_op jit(solution)/shard_map/psum | solution.py:37
  81.6 23.9 %all-reduce.3.cloned.1.call-done = f32[256,2,4,128]{3,2,1,0:T(4,128)} async-done(((f32[256,2,4,128]{3,2,1,0:T(4,128)}), f32[256,2,4,128]{3,2,1,0:T(4,128)}) %all-reduce.3.cloned.1.call-update) | async-done | bytes 1048592 | tf_op jit(solution)/shard_map/psum | solution.py:37
  105.5 1.8 divide_convert_fusion
  107.3 0.4 reshape.80
  107.7 7.7 %fusion.30 = f32[256,4096]{1,0:T(8,128)} fusion(bf16[256,1024]{1,0:T(8,128)(2,1)S(1)} %reshape.80, bf16[1024,4096]{1,0:T(8,128)(2,1)} %param.17), kind=kOutput, calls=%fused_computation.36 | convolution fusion | flops 2147483648 | bytes 13107200 | tf_op jit(solution)/shard_map/dot_general | solution.py:39
  115.4 0.0 all-reduce.5.cloned.1.call-update
  115.4 154.3 %all-reduce.5.cloned.1.call-done = f32[256,4096]{1,0:T(8,128)} async-done(((f32[256,4096]{1,0:T(8,128)}), f32[256,4096]{1,0:T(8,128)}) %all-reduce.5.cloned.1.call-update) | async-done | bytes 4194320 | tf_op jit(solution)/shard_map/psum | solution.py:40
  269.7 4.7 %fusion.3 = bf16[256,4096]{1,0:T(8,128)(2,1)} fusion(f32[256,4096]{1,0:T(8,128)} %all-reduce.5.cloned.1.call-done, bf16[256,4096]{1,0:T(8,128)(2,1)} %param.9), kind=kLoop, calls=%fused_computation.8 | loop fusion | flops 3145728 | bytes 8388608 | tf_op jit(solution)/shard_map/convert_element_type | solution.py:41
  (2 shorter events, 0.0 us)
Async XLA Ops:
  7.2 3.0 %copy-start = (bf16[4096,256]{1,0:T(8,128)(2,1)S(1)}, bf16[4096,256]{1,0:T(8,128)(2,1)}, u32[]{:S(2)}) copy-start(bf16[4096,256]{1,0:T(8,128)(2,1)} %param.15) | copy-start | bytes 6291460
  7.2 98.4 %all-reduce.3.cloned.1.call-start = ((), (), s32[]{:S(2)}) async-start(), calls=%async_computation | async-start | bytes 2097152 | tf_op jit(solution)/shard_map/psum | solution.py:37
  16.5 6.8 %copy-start.2 = (s32[256]{0:T(256)S(1)}, s32[256]{0:T(256)}, u32[]{:S(2)}) copy-start(s32[256]{0:T(256)} %param.10) | copy-start | bytes 3076
  37.3 2.0 copy-start.1
  66.5 203.1 %all-reduce.5.cloned.1.call-start = ((), (), s32[]{:S(2)}) async-start(), calls=%async_computation.1 | async-start | bytes 8388608 | tf_op jit(solution)/shard_map/psum | solution.py:40
Sparse Core Ops, SparseCore 0:
  66.7 38.8 all-reduce.2
  115.5 154.1 all-reduce.4
where the time goes:
time: 282 us; the launch traced here: 281 us
  waiting for transfers between devices  178 us (63%)
  blocking collectives  31.2 us (11%)
  matrix products  28.5 us (10%)
  other arithmetic  26.1 us (9%)
  between operations  14.2 us (5%)
  local copies, waits for them, and re-layouts  2.99 us (1%)
    psum x1, waiting for transfers between devices, local_step(): head_sum = lax.psum(part_out, 'tp')  154 us
    psum x1, waiting for transfers between devices, local_step(): lax.psum((local_acc * rescale, local_denom * rescale), 'sp')  23.9 us
    pmax x1, blocking collectives, local_step(): global_peak = lax.pmax(local_peak, 'sp')  16.2 us
    psum x1, blocking collectives, local_step(): lax.psum((local_acc * rescale, local_denom * rescale), 'sp')  15 us
    select_n x1, other arithmetic, local_step(): jnp.where(at_slot, new_key.reshape(batch, 1, kv_local, head_dim), k_cache)  13.8 us
    dot_general x1, matrix products, local_step(): part_out = jnp.dot(attn_out, w_out, preferred_element_type=jnp.float32)  7.69 us
    dot_general x1, matrix products, local_step(): jnp.dot(normed, w_query, preferred_element_type=jnp.float32)  6.41 us
  transfers between devices with their start and end apart: 2, of which 2 were waited for; matrix products, arithmetic and copies ran while one was open for 0% of the time, Pallas kernels for 0%

commit v1 on v0

--- a/solution.py
+++ b/solution.py
@@ -1,10 +1,229 @@
+import functools
+
 import jax
 import jax.numpy as jnp
 from jax import lax
+from jax.experimental import pallas as pl
+from jax.experimental.pallas import tpu as pltpu
 from jax.sharding import PartitionSpec as P
 
 EPS = 1e-6
 NEG_BIG = -1e30
+MESH = pl.DeviceIdType.MESH
+HALVES = 2
+COLS = 512
+
+
+def combine_kernel(acc_ref, stats_ref, hid_ref, w_hbm, out_ref, w_ref, stat_in, fac_ref, d2d_in, y_out, y_in, obuf, pbuf,
+                   pe_in, abuf, mb_in, fall, w_sem, st_s, st_r, dd_s, dd_r, yy_s, yy_r, p_s, p_r, a_s, a_r, fz_s, fz_r,
+                   fy_s, fy_r, fs_s, fs_r, gs_s, gs_r):
+    heads = acc_ref.shape[1] // 128
+    rows = obuf.shape[1]
+    own_rows = HALVES * rows
+    per_half = out_ref.shape[1] // COLS
+    chunks = HALVES * per_half
+    sp = lax.axis_index('sp')
+    z = lax.axis_index('tp')
+    y, c = sp // 2, sp % 2
+    sib, yn, diag = 2 * y + (1 - c), 2 * (1 - y) + c, 2 * (1 - y) + (1 - c)
+    inner = jnp.logical_or(z == 1, z == 2)
+    is_end = jnp.logical_or(z == 0, z == 3)
+    low = z // 2
+    end_z = low * 3
+    mid_z = 2 - low
+    inner_z = 1 + low
+
+    pltpu.make_async_copy(w_hbm, w_ref, w_sem).start()
+
+    barrier = pltpu.get_barrier_semaphore()
+    for peer in (sib, yn, diag):
+        pl.semaphore_signal(barrier, inc=1, device_id={'sp': peer}, device_id_type=MESH)
+
+    @pl.when(inner)
+    def _():
+        pl.semaphore_signal(barrier, inc=1, device_id={'tp': end_z}, device_id_type=MESH)
+        pl.semaphore_signal(barrier, inc=1, device_id={'tp': mid_z}, device_id_type=MESH)
+        pl.semaphore_wait(barrier, 5)
+
+    @pl.when(is_end)
+    def _():
+        pl.semaphore_signal(barrier, inc=1, device_id={'tp': inner_z}, device_id_type=MESH)
+        pl.semaphore_wait(barrier, 4)
+
+    def remote(src, dst, send, recv, **where):
+        return pltpu.make_async_remote_copy(src_ref=src, dst_ref=dst, send_sem=send, recv_sem=recv, device_id=where,
+                                            device_id_type=MESH)
+
+    def stat_copy(i, peer):
+        lanes = pl.ds(pl.multiple_of((peer % 2) * 2 * own_rows, 128), 2 * own_rows)
+        return remote(stats_ref.at[:, lanes], stat_in.at[i], st_s.at[i], st_r.at[i], sp=peer)
+
+    stat_copies = [stat_copy(i, peer) for i, peer in enumerate((sib, yn, diag))]
+    for copy in stat_copies:
+        copy.start()
+
+    def d2d_copy(t, r):
+        plane = (1 - y) if t == 0 else y
+        start = pl.multiple_of((1 - c) * 2 * own_rows + plane * own_rows + r * rows, rows)
+        return remote(acc_ref.at[pl.ds(start, rows), :], d2d_in.at[t, r], dd_s.at[2 * r + t], dd_r.at[2 * r + t], sp=sib)
+
+    d2d_copies = [[d2d_copy(t, r) for r in range(HALVES)] for t in range(2)]
+    for r in range(HALVES):
+        for t in range(2):
+            d2d_copies[t][r].start()
+
+    for copy in stat_copies:
+        copy.wait()
+    lanes = pl.ds(pl.multiple_of(c * 2 * own_rows, 128), 2 * own_rows)
+    peaks = [stats_ref[0:heads, lanes]] + [stat_in[i, 0:heads, :] for i in range(3)]
+    sums = [stats_ref[heads:2 * heads, lanes]] + [stat_in[i, heads:2 * heads, :] for i in range(3)]
+    top = jnp.maximum(jnp.maximum(peaks[0], peaks[1]), jnp.maximum(peaks[2], peaks[3]))
+    weights = [jnp.exp(peak - top) for peak in peaks]
+    total = sums[0] * weights[0] + sums[1] * weights[1] + (sums[2] * weights[2] + sums[3] * weights[3])
+    factors = jnp.concatenate(
+        [weights[0] / total, weights[1] / total, jnp.zeros((2 * own_rows - 2 * heads, 2 * own_rows), jnp.float32)], axis=0)
+    fac_ref[...] = factors.T
+
+    def combined(t, r, j):
+        plane = (1 - y) if t == 0 else y
+        base = pl.multiple_of(plane * own_rows + r * rows, rows)
+        start = pl.multiple_of(c * 2 * own_rows + base, rows)
+        cols = slice(j * 128, (j + 1) * 128)
+        mine = acc_ref[pl.ds(start, rows), cols] * fac_ref[pl.ds(base, rows), j:j + 1]
+        return mine + d2d_in[t, r, :, cols] * fac_ref[pl.ds(base, rows), heads + j:heads + j + 1]
+
+    def y_copy(r):
+        return remote(y_out.at[r], y_in.at[r], yy_s.at[r], yy_r.at[r], sp=yn)
+
+    y_copies = [y_copy(r) for r in range(HALVES)]
+    for r in range(HALVES):
+        d2d_copies[0][r].wait()
+        for j in range(heads):
+            y_out[r, :, j * 128:(j + 1) * 128] = combined(0, r, j)
+        y_copies[r].start()
+
+    def p_copy(k):
+        return remote(pbuf.at[k], pe_in.at[k], p_s.at[k], p_r.at[k], tp=inner_z)
+
+    def a_copy(k):
+        return remote(abuf.at[k], mb_in.at[k], a_s.at[k], a_r.at[k], tp=mid_z)
+
+    def fz_copy(k):
+        return remote(fall.at[sp, k], fall.at[sp, k], fz_s.at[k], fz_r.at[k], tp=end_z)
+
+    def fy_copy(k, owner):
+        return remote(fall.at[owner, k], fall.at[owner, k], fy_s.at[k], fy_r.at[k], sp=yn)
+
+    def fs_copy(k, owner):
+        return remote(fall.at[owner, k], fall.at[owner, k], fs_s.at[k], fs_r.at[k], sp=sib)
+
+    def gs_copy(k, owner):
+        return remote(fall.at[owner, k], fall.at[owner, k], gs_s.at[k], gs_r.at[k], sp=sib)
+
+    for r in range(HALVES):
+        d2d_copies[1][r].wait()
+        y_copies[r].wait()
+        for j in range(heads):
+            obuf[r, :, j * 128:(j + 1) * 128] = (combined(1, r, j) + y_in[r, :, j * 128:(j + 1) * 128]).astype(jnp.bfloat16)
+        if r == 0:
+            pltpu.make_async_copy(w_hbm, w_ref, w_sem).wait()
+        for j in range(per_half):
+            k = r * per_half + j
+            pbuf[k] = jnp.dot(obuf[r], w_ref[:, j * COLS:(j + 1) * COLS], preferred_element_type=jnp.float32)
+
+            @pl.when(is_end)
+            def _():
+                p_copy(k).start()
+
+    def stage_a(k):
+        @pl.when(inner)
+        def _():
+            p_copy(k).wait_recv()
+            abuf[k] = pbuf[k] + pe_in[k]
+            a_copy(k).start()
+
+    def stage_f(k):
+        @pl.when(inner)
+        def _():
+            a_copy(k).wait_recv()
+            fall[sp, k] = abuf[k] + mb_in[k]
+            fz_copy(k).start()
+
+        @pl.when(is_end)
+        def _():
+            fz_copy(k).wait_recv()
+
+        fy_copy(k, sp).start()
+        fs_copy(k, sp).start()
+
+    def stage_y(k):
+        fy_copy(k, yn).wait_recv()
+        gs_copy(k, yn).start()
+
+    def stage_o(k):
+        fs_copy(k, sib).wait_recv()
+        gs_copy(k, diag).wait_recv()
+        r, j = k // per_half, k % per_half
+        cols = slice(j * COLS, (j + 1) * COLS)
+        for owner in range(4):
+            oy, oc = owner // 2, owner % 2
+            start = oc * 2 * own_rows + oy * own_rows + r * rows
+            out_ref[start:start + rows, cols] = (
+                hid_ref[start:start + rows, cols].astype(jnp.float32) + fall[owner, k]).astype(jnp.bfloat16)
+
+    stages = ((stage_a, 0), (stage_f, 2), (stage_y, 4), (stage_o, 6))
+    for step in range(chunks + 6):
+        for stage, lag in stages:
+            if 0 <= step - lag < chunks:
+                stage(step - lag)
+
+    for k in range(chunks):
+        @pl.when(inner)
+        def _():
+            a_copy(k).wait_send()
+            fz_copy(k).wait_send()
+
+        @pl.when(is_end)
+        def _():
+            p_copy(k).wait_send()
+
+        fy_copy(k, sp).wait_send()
+        fs_copy(k, sp).wait_send()
+        gs_copy(k, yn).wait_send()
+
+
+def combine(acc, stats, hidden, w_out):
+    batch, width = acc.shape
+    features = w_out.shape[1]
+    rows = batch // (4 * HALVES)
+    chunks = HALVES * (features // COLS)
+    dma = lambda *shape: pltpu.SemaphoreType.DMA(shape)
+    f32 = lambda *shape: pltpu.VMEM(shape, jnp.float32)
+    vmem = pl.BlockSpec(memory_space=pltpu.VMEM)
+    return pl.pallas_call(
+        combine_kernel,
+        out_shape=jax.ShapeDtypeStruct((batch, features), jnp.bfloat16),
+        in_specs=[vmem, vmem, vmem, pl.BlockSpec(memory_space=pl.ANY)],
+        out_specs=vmem,
+        scratch_shapes=[
+            pltpu.VMEM(w_out.shape, jnp.bfloat16),
+            f32(3, stats.shape[0], batch // 2),
+            f32(batch // 2, batch // 2),
+            f32(2, HALVES, rows, width),
+            f32(HALVES, rows, width),
+            f32(HALVES, rows, width),
+            pltpu.VMEM((HALVES, rows, width), jnp.bfloat16),
+            f32(chunks, rows, COLS),
+            f32(chunks, rows, COLS),
+            f32(chunks, rows, COLS),
+            f32(chunks, rows, COLS),
+            f32(4, chunks, rows, COLS),
+            pltpu.SemaphoreType.DMA,
+            dma(3), dma(3), dma(2 * HALVES), dma(2 * HALVES), dma(HALVES), dma(HALVES),
+        ] + [dma(chunks)] * 12,
+        compiler_params=pltpu.CompilerParams(collective_id=0, has_side_effects=True, vmem_limit_bytes=60 * 2**20),
+        name='combine',
+    )(acc, stats, hidden, w_out)
 
 
 def solution(mesh):
@@ -32,13 +251,8 @@
         exp_vals = jnp.where(valid, jnp.exp(scores - local_peak), 0.0)
         local_denom = jnp.sum(exp_vals, axis=-1, keepdims=True)
         local_acc = jnp.einsum('bkgt,btkd->bkgd', exp_vals.astype(jnp.bfloat16), v_new, preferred_element_type=jnp.float32)
-        global_peak = lax.pmax(local_peak, 'sp')
-        rescale = jnp.exp(local_peak - global_peak)
-        total_acc, total_denom = lax.psum((local_acc * rescale, local_denom * rescale), 'sp')
-        attn_out = (total_acc / total_denom).astype(jnp.bfloat16).reshape(batch, heads_local * head_dim)
-        part_out = jnp.dot(attn_out, w_out, preferred_element_type=jnp.float32)
-        head_sum = lax.psum(part_out, 'tp')
-        hidden_out = (hid_f32 + head_sum).astype(jnp.bfloat16)
+        stats = jnp.concatenate([local_peak.reshape(batch, heads_local), local_denom.reshape(batch, heads_local)], axis=1).T
+        hidden_out = combine(local_acc.reshape(batch, heads_local * head_dim), stats, hidden, w_out)
         return hidden_out, k_new, v_new
 
     return jax.shard_map(

time: 282 us -> 107 us (0.38)
  waiting for transfers between devices: 178 us -> 0 us
  Pallas kernels: 0 us -> 55.5 us
  blocking collectives: 31.2 us -> 0 us
  between operations: 14.2 us -> 0.75 us
  matrix products: 28.5 us -> 20.7 us
  local copies, waits for them, and re-layouts: 2.99 us -> 8.61 us
  other arithmetic: 26.1 us -> 20.6 us
    psum x2 -> x0, waiting for transfers between devices: 178 us -> none  [the longest x1 154 us: local_step(): head_sum = lax.psum(part_out, 'tp')]
    pallas_call x0 -> x1, Pallas kernels: none -> 55.5 us  [combine(): pl.pallas_call(combine_kernel, out_shape=jax.ShapeDtypeStruct((batch, fea...]
    pmax x1 -> x0, blocking collectives: 16.2 us -> none  [local_step(): global_peak = lax.pmax(local_peak, 'sp')]
    psum x1 -> x0, blocking collectives: 15 us -> none  [local_step(): lax.psum((local_acc * rescale, local_denom * rescale), 'sp')]
    dot_general x1 -> x0, matrix products: 7.69 us -> none  [local_step(): part_out = jnp.dot(attn_out, w_out, preferred_element_type=jnp.float32)]
    convert_element_type x2 -> x0, other arithmetic: 6.5 us -> none  [the longest x1 4.75 us: local_step(): hidden_out = (hid_f32 + head_sum).astype(jnp.bfloat16)]
    unnamed x6 -> x5, local copies, waits for them, and re-layouts: 2.02 us -> 5.15 us
  transfers between devices with their start and end apart: 2 -> 0, of which waited for: 2 -> 0; matrix products, arithmetic and copies ran while one was open for 0% -> 0% of each run, Pallas kernels for 0% -> 0%
where the time goes in v1:
time: 107 us; the launch traced here: 106 us
  Pallas kernels  55.5 us (52%)
  matrix products  20.7 us (19%)
  other arithmetic  20.6 us (19%)
  local copies, waits for them, and re-layouts  8.61 us (8%)
    pallas_call x1, Pallas kernels, combine(): pl.pallas_call(combine_kernel, out_shape=jax.ShapeDtypeStruct((batch, fea...  55.5 us
    select_n x1, other arithmetic, local_step(): jnp.where(at_slot, new_key.reshape(batch, 1, kv_local, head_dim), k_cache)  13.8 us
    dot_general x1, matrix products, local_step(): jnp.dot(normed, w_query, preferred_element_type=jnp.float32)  6.4 us
    unnamed x5, local copies, waits for them, and re-layouts  5.15 us
    dot_general x1, matrix products, local_step(): jnp.einsum('bkgt,btkd->bkgd', exp_vals.astype(jnp.bfloat16), v_new, prefe...  4.78 us
    dot_general x1, matrix products, local_step(): jnp.einsum('bkgd,btkd->bkgt', query, k_new, preferred_element_type=jnp.fl...  3.41 us
    dot_general x1, matrix products, local_step(): jnp.dot(normed, w_value, preferred_element_type=jnp.float32)  3.37 us
    dot_general x1, matrix products, local_step(): jnp.dot(normed, w_key, preferred_element_type=jnp.float32)  2.74 us

profile of v1, /device:TPU:0, one launch (start us, length us, event | category | flops | bytes accessed | tf_op | source)
XLA Modules:
  0.0 106.2 jit_solution(5531559633936838867)
XLA Ops:
  0.6 0.0 copy-start
  0.7 2.2 %fusion = f32[256]{0:T(256)S(1)} fusion(bf16[256,4096]{1,0:T(8,128)(2,1)} %hid_ref.1), kind=kLoop, calls=%fused_computation.4 | loop fusion | flops 3145472 | bytes 2098176 | tf_op jit(solution)/shard_map/reduce_sum | solution.py:237
  2.9 0.7 convert_element_type.22
  3.6 0.8 broadcast_compare_fusion.1
  4.4 0.0 copy-done
  4.4 2.7 %convolution_convert_fusion.2 = bf16[256,256]{0,1:T(8,128)(2,1)S(1)} fusion(bf16[4096,256]{1,0:T(8,128)(2,1)S(1)} %copy-done, bf16[256,4096]{1,0:T(8,128)(2,1)} %hid_ref.1, f32[4096]{0:T(1024)S(1)} %convert_element_type.22, f32[256]{0:T(256)S(1)} %add_rsqrt_fusion), kind=kOutput, calls=%fused_computation.15 | convolution fusion | flops 541130752 | bytes 4342784 | tf_op jit(solution)/shard_map/dot_general | solution.py:241
  7.1 0.1 copy.17
  7.3 3.4 %convolution_convert_fusion.1 = bf16[256,256]{0,1:T(8,128)(2,1)S(1)} fusion(bf16[4096,256]{1,0:T(8,128)(2,1)} %param.16, bf16[256,4096]{1,0:T(8,128)(2,1)} %hid_ref.1, f32[4096]{0:T(1024)S(1)} %convert_element_type.22, f32[256]{0:T(256)S(1)} %add_rsqrt_fusion), kind=kOutput, calls=%fused_computation.14 | convolution fusion | flops 541130752 | bytes 4342784 | tf_op jit(solution)/shard_map/dot_general | solution.py:242
  10.6 0.1 copy.19
  10.8 6.4 %convolution_convert_fusion = bf16[256,1024]{1,0:T(8,128)(2,1)S(1)} fusion(bf16[4096,1024]{1,0:T(8,128)(2,1)} %param.14, bf16[256,4096]{1,0:T(8,128)(2,1)} %hid_ref.1, f32[4096]{0:T(1024)S(1)} %convert_element_type.22, f32[256]{0:T(256)S(1)} %add_rsqrt_fusion), kind=kOutput, calls=%fused_computation.12 | convolution fusion | flops 2151940096 | bytes 11027456 | tf_op jit(solution)/shard_map/dot_general | solution.py:239
  17.2 0.4 reshape.79
  17.6 13.8 %broadcast_select_fusion.1 = (bf16[256,32,2,128]{3,2,1,0:T(2,128)(2,1)S(1)}, bf16[256,32,2,128]{3,2,1,0:T(2,128)(2,1)}) fusion(bf16[256,32,2,128]{3,2,1,0:T(2,128)(2,1)} %param.11, pred[256,32]{1,0:T(8,128)(4,1)S(1)} %get-tuple-element.6, bf16[256,2,128]{2,1,0:T(2,128)(2,1)S(1)} %copy.17, bf16[256,32,2,128]{3,2,1,0:T(2,128)(2,1)} %param.12, ...), kind=kLoop, calls=%fused_computation.1 | loop fusion | flops 4194304 | bytes 17047552 | tf_op jit(solution)/shard_map/jit(_where)/select_n | solution.py:245
  31.3 0.0 copy-start.1
  31.4 2.0 %copy-done.1 = bf16[256,32,2,128]{3,2,1,0:T(2,128)(2,1)} copy-done((bf16[256,32,2,128]{3,2,1,0:T(2,128)(2,1)}, bf16[256,32,2,128]{3,2,1,0:T(2,128)(2,1)S(1)}, u32[]{:S(2)}) %copy-start.1) | copy-done | bytes 4194328
  33.4 3.4 %fusion.23 = (f32[256,2,4]{2,1,0:T(2,128)S(1)}, f32[256,2,4,32]{3,2,1,0:T(4,128)}) fusion(bf16[256,2,4,128]{3,2,1,0:T(4,128)(2,1)S(1)} %reshape.79, bf16[256,32,2,128]{3,2,1,0:T(2,128)(2,1)S(1)} %get-tuple-element.13, pred[256,32]{1,0:T(8,128)(4,1)S(1)} %get-tuple-element.5), kind=kOutput, calls=%fused_computation.28 | convolution fusion | flops 16971776 | bytes 4997120 | tf_op jit(solution)/shard_map/bkgd,btkd->bkgt/dot_general | solution.py:247
  36.8 0.1 copy.21
  36.9 2.5 %fusion.13 = f32[256,2,4]{2,1,0:T(2,128)S(1)} fusion(f32[256,2,4,32]{3,2,1,0:T(4,128)} %get-tuple-element.8, f32[256,2,4]{2,1,0:T(2,128)S(1)} %get-tuple-element.7, pred[256,32]{1,0:T(8,128)(4,1)S(1)} %get-tuple-element.5), kind=kLoop, calls=%fused_computation.17 | loop fusion | flops 194560 | bytes 286720 | tf_op jit(solution)/shard_map/reduce_sum | solution.py:252
  39.4 4.8 %fusion.3 = f32[256,2,4,128]{3,2,1,0:T(4,128)} fusion(bf16[256,32,2,128]{3,2,1,0:T(2,128)(2,1)} %get-tuple-element.14, f32[256,2,4,32]{3,2,1,0:T(4,128)} %get-tuple-element.8, f32[256,2,4]{2,1,0:T(2,128)S(1)} %get-tuple-element.7, pred[256,32]{1,0:T(8,128)(4,1)S(1)} %get-tuple-element.5), kind=kOutput, calls=%fused_computation.7 | convolution fusion | flops 16973824 | bytes 5521408 | tf_op jit(solution)/shard_map/bkgt,btkd->bkgd/dot_general | solution.py:253
  44.2 0.1 copy.22
  44.3 0.6 maximum_bitcast_fusion.stats_ref
  44.9 2.6 %reshape.80.acc_ref = f32[256,1024]{1,0:T(8,128)} reshape(f32[256,2,4,128]{3,2,1,0:T(4,128)} %fusion.3) | data formatting | bytes 2097152 | tf_op jit(solution)/shard_map/reshape | solution.py:255
  47.5 55.5 %combine.1 = bf16[256,4096]{1,0:T(8,128)(2,1)} custom-call(f32[256,1024]{1,0:T(8,128)} %reshape.80.acc_ref, f32[16,256]{1,0:T(8,128)} %maximum_bitcast_fusion.stats_ref, bf16[256,4096]{1,0:T(8,128)(2,1)} %hid_ref.1, bf16[1024,4096]{1,0:T(8,128)(2,1)} %w_hbm.1), custom_call_target="tpu_custom_call" | custom-call | tf_op jit(solution)/shard_map/combine/pallas_call | solution.py:203
  103.0 3.1 %copy.34 = bf16[256,4096]{1,0:T(8,128)(2,1)} copy(bf16[256,4096]{1,0:T(8,128)(2,1)} %combine.1) | data formatting | bytes 4194304
  (4 shorter events, 0.0 us)
Async XLA Ops:
  0.6 3.8 %copy-start = (bf16[4096,256]{1,0:T(8,128)(2,1)S(1)}, bf16[4096,256]{1,0:T(8,128)(2,1)}, u32[]{:S(2)}) copy-start(bf16[4096,256]{1,0:T(8,128)(2,1)} %param.15) | copy-start | bytes 6291460
  31.3 2.0 %copy-start.1 = (bf16[256,32,2,128]{3,2,1,0:T(2,128)(2,1)}, bf16[256,32,2,128]{3,2,1,0:T(2,128)(2,1)S(1)}, u32[]{:S(2)}) copy-start(bf16[256,32,2,128]{3,2,1,0:T(2,128)(2,1)S(1)} %get-tuple-element.13) | copy-start | bytes 12582916

commit v2 on v1

--- a/solution.py
+++ b/solution.py
@@ -1,5 +1,3 @@
-import functools
-
 import jax
 import jax.numpy as jnp
 from jax import lax
@@ -12,6 +10,8 @@
 MESH = pl.DeviceIdType.MESH
 HALVES = 2
 COLS = 512
+BLOCK = 32
+SCALE = 128 ** -0.5
 
 
 def combine_kernel(acc_ref, stats_ref, hid_ref, w_hbm, out_ref, w_ref, stat_in, fac_ref, d2d_in, y_out, y_in, obuf, pbuf,
@@ -226,34 +226,154 @@
     )(acc, stats, hidden, w_out)
 
 
+def attend_kernel(len_smem, len_ref, hid_hbm, gain_ref, wq_hbm, wk_hbm, wv_hbm, k_hbm, v_hbm, kout_hbm, vout_hbm, acc_ref,
+                  stats_ref, hid, nbuf, wq, wk, wv, kbuf, vbuf, qbuf, pair_f32, nk, nv, statbuf, hid_sem, wq_sem, wk_sem, wv_sem,
+                  k_sem, v_sem, ko_sem, vo_sem):
+    batch, features = hid.shape
+    heads = qbuf.shape[1] // 128
+    slots = batch * BLOCK
+    base = lax.axis_index('sp') * BLOCK
+    pieces = k_sem.shape[0]
+    piece = slots // pieces
+    copy = pltpu.make_async_copy
+    quarter = batch // hid_sem.shape[0]
+    hid_copies = [copy(hid_hbm.at[pl.ds(i * quarter, quarter), :], hid.at[pl.ds(i * quarter, quarter), :], hid_sem.at[i])
+                  for i in range(hid_sem.shape[0])]
+    wk_copy, wv_copy = copy(wk_hbm, wk, wk_sem), copy(wv_hbm, wv, wv_sem)
+    wide = wq.shape[2]
+    wq_copies = [copy(wq_hbm.at[:, pl.ds(i * wide, wide)], wq.at[i], wq_sem.at[i]) for i in range(wq.shape[0])]
+    for c in hid_copies + [wk_copy, wv_copy] + wq_copies:
+        c.start()
+
+    def block_copy(src, dst, sem, i, step=piece):
+        rows = pl.ds(pl.multiple_of(i * step, step), step)
+        return copy(src.at[rows], dst.at[rows], sem.at[i])
+
+    for i in range(pieces):
+        block_copy(k_hbm, kbuf, k_sem, i).start()
+        block_copy(v_hbm, vbuf, v_sem, i).start()
+
+    gain = gain_ref[...].astype(jnp.float32)
+
+    def norm_rows(i):
+        rows = pl.ds(pl.multiple_of(i * 16, 16), 16)
+        h = hid[rows, :].astype(jnp.float32)
+        inv_rms = lax.rsqrt(jnp.mean(h * h, axis=-1, keepdims=True) + EPS)
+        nbuf[rows, :] = (h * inv_rms * gain).astype(jnp.bfloat16)
+
+    for i, c in enumerate(hid_copies):
+        c.wait()
+        per = quarter // 16
+        pl.loop(i * per, (i + 1) * per)(norm_rows)
+
+    for weight, weight_copy, out in ((wk, wk_copy, nk), (wv, wv_copy, nv)):
+        weight_copy.wait()
+        new = jnp.dot(nbuf[...], weight[...], preferred_element_type=jnp.float32)
+        for j in range(2):
+            pair_f32[pl.ds(j, batch, stride=2), :] = new[:, j * 128:(j + 1) * 128]
+        out.reshape(2 * batch, 128)[...] = pair_f32[...].astype(jnp.bfloat16)
+
+    for i, c in enumerate(wq_copies):
+        c.wait()
+        query = jnp.dot(nbuf[...], wq[i], preferred_element_type=jnp.float32)
+        qbuf[:, i * wide:(i + 1) * wide] = query.astype(jnp.bfloat16).astype(jnp.float32)
+
+    k_rows, v_rows = kbuf.reshape(kbuf.shape[0] * 2, 128), vbuf.reshape(vbuf.shape[0] * 2, 128)
+    lane = lax.broadcasted_iota(jnp.int32, (8, 128), 1)
+    row = lax.broadcasted_iota(jnp.int32, (8, 128), 0)
+    slot_pos = base + (lane % 64) // 2
+    own_seq = (lane // 64) == (row % 2)
+    even = lane % 2 == 0
+    pairs = [row // 2 == j for j in range(4)]
+
+    def attend_tile(i):
+        seqs = pl.ds(pl.multiple_of(i * 8, 8), 8)
+        keys = pl.ds(pl.multiple_of(i * 512, 512), 512)
+        q = jnp.concatenate([qbuf[seqs, h * 128:(h + 1) * 128] for h in range(heads)], axis=0).astype(jnp.bfloat16)
+        s = lax.dot_general(q, k_rows[keys, :], (((1,), (1,)), ((), ())), preferred_element_type=jnp.float32)
+        valid = jnp.logical_and(own_seq, slot_pos <= len_ref[seqs, :])
+        valids = (jnp.logical_and(valid, even), jnp.logical_and(valid, jnp.logical_not(even)))
+        stat = jnp.zeros((8, 128), jnp.float32)
+        probs = []
+        for h in range(heads):
+            part = [s[h * 8:(h + 1) * 8, j * 128:(j + 1) * 128] for j in range(4)]
+            score = jnp.where(pairs[0], part[0], jnp.where(pairs[1], part[1], jnp.where(pairs[2], part[2], part[3])))
+            ok = valids[h // (heads // 2)]
+            score = jnp.where(ok, score * SCALE, NEG_BIG)
+            peak = jnp.max(score, axis=1, keepdims=True)
+            e = jnp.where(ok, jnp.exp(score - peak), 0.0)
+            stat = jnp.where(lane == h, peak, stat)
+            stat = jnp.where(lane == heads + h, jnp.sum(e, axis=1, keepdims=True), stat)
+            probs.append(jnp.concatenate([jnp.where(pairs[j], e, 0.0) for j in range(4)], axis=1))
+        p = jnp.concatenate(probs, axis=0).astype(jnp.bfloat16)
+        o = jnp.dot(p, v_rows[keys, :], preferred_element_type=jnp.float32)
+        for h in range(heads):
+            acc_ref[seqs, h * 128:(h + 1) * 128] = o[h * 8:(h + 1) * 8, :]
+        statbuf[seqs, :] = stat
+
+    @pl.loop(0, pieces)
+    def _(i):
+        block_copy(k_hbm, kbuf, k_sem, i).wait()
+        block_copy(v_hbm, vbuf, v_sem, i).wait()
+        seqs = piece // BLOCK
+
+        @pl.loop(0, seqs, unroll=8)
+        def _(j):
+            b = i * seqs + j
+            at = len_smem[b] - base
+            slot = jnp.where(jnp.logical_and(at >= 0, at < BLOCK), b * BLOCK + at, slots)
+            kbuf[slot] = nk[b]
+            vbuf[slot] = nv[b]
+
+        @pl.loop(0, seqs // 8, unroll=2)
+        def _(j):
+            attend_tile(i * (seqs // 8) + j)
+
+        block_copy(kbuf, kout_hbm, ko_sem, i).start()
+        block_copy(vbuf, vout_hbm, vo_sem, i).start()
+
+    for i in range(batch // 128):
+        stats_ref[:, i * 128:(i + 1) * 128] = statbuf[i * 128:(i + 1) * 128, :].T[0:2 * heads, :]
+
+    for i in range(pieces):
+        block_copy(kbuf, kout_hbm, ko_sem, i).wait()
+        block_copy(vbuf, vout_hbm, vo_sem, i).wait()
+
+
+def attend(hidden, lengths, k_cache, v_cache, norm_gain, w_query, w_key, w_value):
+    batch, block, kv, dim = k_cache.shape
+    features, width = w_query.shape
+    slots = batch * block
+    bf16 = lambda *shape: pltpu.VMEM(shape, jnp.bfloat16)
+    f32 = lambda *shape: pltpu.VMEM(shape, jnp.float32)
+    dma = lambda *shape: pltpu.SemaphoreType.DMA(shape)
+    vmem, hbm = pl.BlockSpec(memory_space=pltpu.VMEM), pl.BlockSpec(memory_space=pl.ANY)
+    cache = jax.ShapeDtypeStruct((slots, kv, dim), jnp.bfloat16)
+    k_new, v_new, acc, stats = pl.pallas_call(
+        attend_kernel,
+        out_shape=[cache, cache, jax.ShapeDtypeStruct((batch, width), jnp.float32),
+                   jax.ShapeDtypeStruct((2 * width // dim, batch), jnp.float32)],
+        in_specs=[pl.BlockSpec(memory_space=pltpu.SMEM), vmem, hbm, vmem, hbm, hbm, hbm, hbm, hbm],
+        out_specs=[hbm, hbm, vmem, vmem],
+        scratch_shapes=[
+            bf16(batch, features), bf16(batch, features), bf16(width // 256, features, 256), bf16(features, 256),
+            bf16(features, 256), bf16(slots + 8, kv, dim), bf16(slots + 8, kv, dim), f32(batch, width), f32(2 * batch, dim),
+            bf16(batch, kv, dim), bf16(batch, kv, dim), f32(batch, 128),
+            dma(4), dma(width // 256), pltpu.SemaphoreType.DMA, pltpu.SemaphoreType.DMA, dma(8), dma(8), dma(8), dma(8),
+        ],
+        compiler_params=pltpu.CompilerParams(vmem_limit_bytes=60 * 2**20),
+        name='attend',
+    )(lengths, jnp.broadcast_to(lengths[:, None], (batch, 128)), hidden, norm_gain.reshape(1, features), w_query, w_key, w_value,
+      k_cache.reshape(slots, kv, dim), v_cache.reshape(slots, kv, dim))
+    return k_new.reshape(k_cache.shape), v_new.reshape(v_cache.shape), acc, stats
+
+
 def solution(mesh):
     cache_spec = P('dp', 'sp', 'tp', None)
 
     def local_step(hidden, lengths, k_cache, v_cache, norm_gain, w_query, w_key, w_value, w_out):
-        batch, seq_block, kv_local, head_dim = k_cache.shape
-        heads_local = w_query.shape[1] // head_dim
-        group = heads_local // kv_local
-        hid_f32 = hidden.astype(jnp.float32)
-        inv_rms = lax.rsqrt(jnp.mean(hid_f32 * hid_f32, axis=-1, keepdims=True) + EPS)
-        normed = (hid_f32 * inv_rms * norm_gain.astype(jnp.float32)).astype(jnp.bfloat16)
-        query = jnp.dot(normed, w_query, preferred_element_type=jnp.float32).astype(jnp.bfloat16)
-        query = query.reshape(batch, kv_local, group, head_dim)
-        new_key = jnp.dot(normed, w_key, preferred_element_type=jnp.float32).astype(jnp.bfloat16)
-        new_value = jnp.dot(normed, w_value, preferred_element_type=jnp.float32).astype(jnp.bfloat16)
-        positions = lax.axis_index('sp') * seq_block + jnp.arange(seq_block)
-        at_slot = (positions[None, :] == lengths[:, None])[:, :, None, None]
-        k_new = jnp.where(at_slot, new_key.reshape(batch, 1, kv_local, head_dim), k_cache)
-        v_new = jnp.where(at_slot, new_value.reshape(batch, 1, kv_local, head_dim), v_cache)
-        scores = jnp.einsum('bkgd,btkd->bkgt', query, k_new, preferred_element_type=jnp.float32) * (head_dim ** -0.5)
-        valid = (positions[None, :] <= lengths[:, None])[:, None, None, :]
-        scores = jnp.where(valid, scores, NEG_BIG)
-        local_peak = jnp.max(scores, axis=-1, keepdims=True)
-        exp_vals = jnp.where(valid, jnp.exp(scores - local_peak), 0.0)
-        local_denom = jnp.sum(exp_vals, axis=-1, keepdims=True)
-        local_acc = jnp.einsum('bkgt,btkd->bkgd', exp_vals.astype(jnp.bfloat16), v_new, preferred_element_type=jnp.float32)
-        stats = jnp.concatenate([local_peak.reshape(batch, heads_local), local_denom.reshape(batch, heads_local)], axis=1).T
-        hidden_out = combine(local_acc.reshape(batch, heads_local * head_dim), stats, hidden, w_out)
-        return hidden_out, k_new, v_new
+        k_new, v_new, acc, stats = attend(hidden, lengths, k_cache, v_cache, norm_gain, w_query, w_key, w_value)
+        return combine(acc, stats, hidden, w_out), k_new, v_new
 
     return jax.shard_map(
         local_step,

time: 107 us -> 90.2 us (0.84)
  Pallas kernels: 55.5 us -> 83.5 us
  matrix products: 20.7 us -> 0 us
  other arithmetic: 20.6 us -> 0 us
  local copies, waits for them, and re-layouts: 8.61 us -> 5.86 us
    pallas_call x0 -> x1, Pallas kernels: none -> 28 us  [attend(): pl.pallas_call(attend_kernel, out_shape=[cache, cache, jax.ShapeDtypeStru...]
    dot_general x5 -> x0, matrix products: 20.7 us -> none  [the longest x1 6.4 us: local_step(): jnp.dot(normed, w_query, preferred_element_type=jnp.float32)]
    select_n x1 -> x0, other arithmetic: 13.8 us -> none  [local_step(): jnp.where(at_slot, new_key.reshape(batch, 1, kv_local, head_dim), k_cache)]
    reduce_sum x2 -> x0, other arithmetic: 4.71 us -> none  [the longest x1 2.48 us: local_step(): local_denom = jnp.sum(exp_vals, axis=-1, keepdims=True)]
    unnamed x5 -> x1, local copies, waits for them, and re-layouts: 5.15 us -> 3.13 us
    reshape x2 -> x1, local copies, waits for them, and re-layouts: 2.98 us -> 1.3 us  [attend(): norm_gain.reshape(1, features)]
    broadcast_in_dim x2 -> x1, local copies, waits for them, and re-layouts: 0.23 us -> 1.43 us  [attend(): jnp.broadcast_to(lengths[:, None], (batch, 128))]
where the time goes in v2:
time: 90.2 us; the launch traced here: 90 us
  Pallas kernels  83.5 us (93%)
  local copies, waits for them, and re-layouts  5.86 us (6%)
    pallas_call x1, Pallas kernels, combine(): pl.pallas_call(combine_kernel, out_shape=jax.ShapeDtypeStruct((batch, fea...  55.5 us
    pallas_call x1, Pallas kernels, attend(): pl.pallas_call(attend_kernel, out_shape=[cache, cache, jax.ShapeDtypeStru...  28 us
    unnamed x1, local copies, waits for them, and re-layouts  3.13 us

profile of v2, /device:TPU:0, one launch (start us, length us, event | category | flops | bytes accessed | tf_op | source)
XLA Modules:
  0.0 90.0 jit_solution(13146863144636141258)
XLA Ops:
  0.6 1.3 %reshape.22.gain_ref = bf16[1,4096]{1,0:T(2,128)(2,1)} reshape(bf16[4096]{0:T(1024)(128)(2,1)} %param.13) | data formatting | bytes 16384 | tf_op jit(solution)/shard_map/reshape | solution.py:366
  1.9 1.4 %broadcast_in_dim.2.len_ref = s32[256,128]{1,0:T(8,128)} broadcast(s32[256]{0:T(256)} %len_smem.1), dimensions={0} | broadcast | bytes 132096 | tf_op jit(solution)/shard_map/broadcast_in_dim | solution.py:366
  3.4 28.0 %attend.1 = (bf16[8192,2,128]{2,1,0:T(2,128)(2,1)}, bf16[8192,2,128]{2,1,0:T(2,128)(2,1)}, f32[256,1024]{1,0:T(8,128)}, f32[16,256]{1,0:T(8,128)}) custom-call(s32[256]{0:T(256)} %len_smem.1, s32[256,128]{1,0:T(8,128)} %broadcast_in_dim.2.len_ref, bf16[256,4096]{1,0:T(8,128)(2,1)} %hid_ref.1, bf16[1,4096]{1,0:T(2,128)(2,1)} %reshape.22.gain_ref, ...), custom_call_target="tpu_custom_call" | custom-call | tf_op jit(solution)/shard_map/attend/pallas_call | solution.py:352
  31.3 55.5 %combine.1 = bf16[256,4096]{1,0:T(8,128)(2,1)} custom-call(f32[256,1024]{1,0:T(8,128)} %get-tuple-element.7.acc_ref, f32[16,256]{1,0:T(8,128)} %get-tuple-element.8.stats_ref, bf16[256,4096]{1,0:T(8,128)(2,1)} %hid_ref.1, bf16[1024,4096]{1,0:T(8,128)(2,1)} %w_hbm.1), custom_call_target="tpu_custom_call" | custom-call | tf_op jit(solution)/shard_map/combine/pallas_call | solution.py:203
  86.9 3.1 %copy.13 = bf16[256,4096]{1,0:T(8,128)(2,1)} copy(bf16[256,4096]{1,0:T(8,128)(2,1)} %combine.1) | data formatting | bytes 4194304

commit v3 on v2

--- a/solution.py
+++ b/solution.py
@@ -12,10 +12,13 @@
 COLS = 512
 BLOCK = 32
 SCALE = 128 ** -0.5
-
-
-def combine_kernel(acc_ref, stats_ref, hid_ref, w_hbm, out_ref, w_ref, stat_in, fac_ref, d2d_in, y_out, y_in, obuf, pbuf,
-                   pe_in, abuf, mb_in, fall, w_sem, st_s, st_r, dd_s, dd_r, yy_s, yy_r, p_s, p_r, a_s, a_r, fz_s, fz_r,
+UNROLL = 2
+ATTEND_VMEM = 62.5
+COMBINE_VMEM = 60.5
+
+
+def combine_kernel(acc_ref, stats_ref, hid_hbm, w_hbm, out_ref, hid_ref, w_ref, stat_in, fac_ref, d2d_in, y_out, y_in, obuf, pbuf,
+                   pe_in, abuf, mb_in, fall, h_sem, w_sem, st_s, st_r, dd_s, dd_r, yy_s, yy_r, p_s, p_r, a_s, a_r, fz_s, fz_r,
                    fy_s, fy_r, fs_s, fs_r, gs_s, gs_r):
     heads = acc_ref.shape[1] // 128
     rows = obuf.shape[1]
@@ -33,7 +36,9 @@
     mid_z = 2 - low
     inner_z = 1 + low
 
-    pltpu.make_async_copy(w_hbm, w_ref, w_sem).start()
+    hid_copy, w_copy = pltpu.make_async_copy(hid_hbm, hid_ref, h_sem), pltpu.make_async_copy(w_hbm, w_ref, w_sem)
+    w_copy.start()
+    hid_copy.start()
 
     barrier = pltpu.get_barrier_semaphore()
     for peer in (sib, yn, diag):
@@ -121,12 +126,13 @@
         return remote(fall.at[owner, k], fall.at[owner, k], gs_s.at[k], gs_r.at[k], sp=sib)
 
     for r in range(HALVES):
+        if r == 0:
+            w_copy.wait()
+            hid_copy.wait()
         d2d_copies[1][r].wait()
         y_copies[r].wait()
         for j in range(heads):
             obuf[r, :, j * 128:(j + 1) * 128] = (combined(1, r, j) + y_in[r, :, j * 128:(j + 1) * 128]).astype(jnp.bfloat16)
-        if r == 0:
-            pltpu.make_async_copy(w_hbm, w_ref, w_sem).wait()
         for j in range(per_half):
             k = r * per_half + j
             pbuf[k] = jnp.dot(obuf[r], w_ref[:, j * COLS:(j + 1) * COLS], preferred_element_type=jnp.float32)
@@ -199,13 +205,14 @@
     chunks = HALVES * (features // COLS)
     dma = lambda *shape: pltpu.SemaphoreType.DMA(shape)
     f32 = lambda *shape: pltpu.VMEM(shape, jnp.float32)
-    vmem = pl.BlockSpec(memory_space=pltpu.VMEM)
+    vmem, hbm = pl.BlockSpec(memory_space=pltpu.VMEM), pl.BlockSpec(memory_space=pltpu.HBM)
     return pl.pallas_call(
         combine_kernel,
         out_shape=jax.ShapeDtypeStruct((batch, features), jnp.bfloat16),
-        in_specs=[vmem, vmem, vmem, pl.BlockSpec(memory_space=pl.ANY)],
+        in_specs=[vmem, vmem, hbm, hbm],
         out_specs=vmem,
         scratch_shapes=[
+            pltpu.VMEM(hidden.shape, jnp.bfloat16),
             pltpu.VMEM(w_out.shape, jnp.bfloat16),
             f32(3, stats.shape[0], batch // 2),
             f32(batch // 2, batch // 2),
@@ -218,23 +225,22 @@
             f32(chunks, rows, COLS),
             f32(chunks, rows, COLS),
             f32(4, chunks, rows, COLS),
-            pltpu.SemaphoreType.DMA,
-            dma(3), dma(3), dma(2 * HALVES), dma(2 * HALVES), dma(HALVES), dma(HALVES),
+            pltpu.SemaphoreType.DMA, pltpu.SemaphoreType.DMA, dma(3), dma(3), dma(2 * HALVES), dma(2 * HALVES), dma(HALVES), dma(HALVES),
         ] + [dma(chunks)] * 12,
-        compiler_params=pltpu.CompilerParams(collective_id=0, has_side_effects=True, vmem_limit_bytes=60 * 2**20),
+        compiler_params=pltpu.CompilerParams(collective_id=0, has_side_effects=True, vmem_limit_bytes=int(COMBINE_VMEM * 2**20)),
         name='combine',
     )(acc, stats, hidden, w_out)
 
 
-def attend_kernel(len_smem, len_ref, hid_hbm, gain_ref, wq_hbm, wk_hbm, wv_hbm, k_hbm, v_hbm, kout_hbm, vout_hbm, acc_ref,
-                  stats_ref, hid, nbuf, wq, wk, wv, kbuf, vbuf, qbuf, pair_f32, nk, nv, statbuf, hid_sem, wq_sem, wk_sem, wv_sem,
-                  k_sem, v_sem, ko_sem, vo_sem):
+def attend_kernel(len_ref, hid_hbm, gain_ref, wq_hbm, wk_hbm, wv_hbm, k_hbm, v_hbm, kout_hbm, vout_hbm, acc_ref, stats_ref,
+                  hid, nbuf, wq, wk, wv, kbuf, vbuf, qbuf, nk, nv, statbuf, hid_sem, wq_sem, wk_sem, wv_sem, k_sem, v_sem,
+                  ko_sem, vo_sem):
     batch, features = hid.shape
     heads = qbuf.shape[1] // 128
-    slots = batch * BLOCK
     base = lax.axis_index('sp') * BLOCK
     pieces = k_sem.shape[0]
-    piece = slots // pieces
+    seqs = batch // pieces
+    piece = seqs * BLOCK * 2
     copy = pltpu.make_async_copy
     quarter = batch // hid_sem.shape[0]
     hid_copies = [copy(hid_hbm.at[pl.ds(i * quarter, quarter), :], hid.at[pl.ds(i * quarter, quarter), :], hid_sem.at[i])
@@ -242,18 +248,15 @@
     wk_copy, wv_copy = copy(wk_hbm, wk, wk_sem), copy(wv_hbm, wv, wv_sem)
     wide = wq.shape[2]
     wq_copies = [copy(wq_hbm.at[:, pl.ds(i * wide, wide)], wq.at[i], wq_sem.at[i]) for i in range(wq.shape[0])]
-    for c in hid_copies + [wk_copy, wv_copy] + wq_copies:
+
+    def block_copy(src, dst, sem, i):
+        rows = pl.ds(pl.multiple_of(i * piece, piece), piece)
+        return copy(src.at[rows, :], dst.at[rows, :], sem.at[i])
+
+    for c in hid_copies + [wk_copy, wv_copy]:
         c.start()
 
-    def block_copy(src, dst, sem, i, step=piece):
-        rows = pl.ds(pl.multiple_of(i * step, step), step)
-        return copy(src.at[rows], dst.at[rows], sem.at[i])
-
-    for i in range(pieces):
-        block_copy(k_hbm, kbuf, k_sem, i).start()
-        block_copy(v_hbm, vbuf, v_sem, i).start()
-
-    gain = gain_ref[...].astype(jnp.float32)
+    gain = gain_ref[...].astype(jnp.float32).reshape(1, features)
 
     def norm_rows(i):
         rows = pl.ds(pl.multiple_of(i * 16, 16), 16)
@@ -263,35 +266,57 @@
 
     for i, c in enumerate(hid_copies):
         c.wait()
+        if i == 0:
+            for w in wq_copies:
+                w.start()
+        if i == 1:
+            for j in range(pieces):
+                block_copy(k_hbm, kbuf, k_sem, j).start()
+                block_copy(v_hbm, vbuf, v_sem, j).start()
         per = quarter // 16
         pl.loop(i * per, (i + 1) * per)(norm_rows)
 
     for weight, weight_copy, out in ((wk, wk_copy, nk), (wv, wv_copy, nv)):
         weight_copy.wait()
         new = jnp.dot(nbuf[...], weight[...], preferred_element_type=jnp.float32)
+        new = new.astype(jnp.bfloat16).astype(jnp.float32)
         for j in range(2):
-            pair_f32[pl.ds(j, batch, stride=2), :] = new[:, j * 128:(j + 1) * 128]
-        out.reshape(2 * batch, 128)[...] = pair_f32[...].astype(jnp.bfloat16)
+            out[j] = new[:, j * 128:(j + 1) * 128]
 
     for i, c in enumerate(wq_copies):
         c.wait()
         query = jnp.dot(nbuf[...], wq[i], preferred_element_type=jnp.float32)
         qbuf[:, i * wide:(i + 1) * wide] = query.astype(jnp.bfloat16).astype(jnp.float32)
 
-    k_rows, v_rows = kbuf.reshape(kbuf.shape[0] * 2, 128), vbuf.reshape(vbuf.shape[0] * 2, 128)
     lane = lax.broadcasted_iota(jnp.int32, (8, 128), 1)
     row = lax.broadcasted_iota(jnp.int32, (8, 128), 0)
     slot_pos = base + (lane % 64) // 2
     own_seq = (lane // 64) == (row % 2)
     even = lane % 2 == 0
     pairs = [row // 2 == j for j in range(4)]
+    odd_row = row % 2 == 1
+    slot_row = lax.broadcasted_iota(jnp.int32, (16, 128), 0) // 2
+
+    def place_new(b):
+        at = len_ref[b] - base
+        first = jnp.clip(at, 0, BLOCK - 1) // 8
+        rows = pl.ds(pl.multiple_of(b * 2 * BLOCK + first * 16, 16), 16)
+        here = slot_row == at - first * 8
+        for buf, new in ((kbuf, nk), (vbuf, nv)):
+            fresh = jnp.where(odd_row, jnp.broadcast_to(new[1, pl.ds(b, 1), :], (8, 128)),
+                              jnp.broadcast_to(new[0, pl.ds(b, 1), :], (8, 128)))
+            fresh = jnp.concatenate([fresh, fresh], axis=0)
+            buf[rows, :] = jnp.where(here, fresh, buf[rows, :].astype(jnp.float32)).astype(jnp.bfloat16)
 
     def attend_tile(i):
-        seqs = pl.ds(pl.multiple_of(i * 8, 8), 8)
+        seq8 = pl.ds(pl.multiple_of(i * 8, 8), 8)
         keys = pl.ds(pl.multiple_of(i * 512, 512), 512)
-        q = jnp.concatenate([qbuf[seqs, h * 128:(h + 1) * 128] for h in range(heads)], axis=0).astype(jnp.bfloat16)
-        s = lax.dot_general(q, k_rows[keys, :], (((1,), (1,)), ((), ())), preferred_element_type=jnp.float32)
-        valid = jnp.logical_and(own_seq, slot_pos <= len_ref[seqs, :])
+        q = jnp.concatenate([qbuf[seq8, h * 128:(h + 1) * 128] for h in range(heads)], axis=0).astype(jnp.bfloat16)
+        s = lax.dot_general(q, kbuf[keys, :], (((1,), (1,)), ((), ())), preferred_element_type=jnp.float32)
+        lens = jnp.full((8, 128), len_ref[i * 8], jnp.int32)
+        for j in range(1, 8):
+            lens = jnp.where(row == j, len_ref[i * 8 + j], lens)
+        valid = jnp.logical_and(own_seq, slot_pos <= lens)
         valids = (jnp.logical_and(valid, even), jnp.logical_and(valid, jnp.logical_not(even)))
         stat = jnp.zeros((8, 128), jnp.float32)
         probs = []
@@ -306,26 +331,21 @@
             stat = jnp.where(lane == heads + h, jnp.sum(e, axis=1, keepdims=True), stat)
             probs.append(jnp.concatenate([jnp.where(pairs[j], e, 0.0) for j in range(4)], axis=1))
         p = jnp.concatenate(probs, axis=0).astype(jnp.bfloat16)
-        o = jnp.dot(p, v_rows[keys, :], preferred_element_type=jnp.float32)
+        o = jnp.dot(p, vbuf[keys, :], preferred_element_type=jnp.float32)
         for h in range(heads):
-            acc_ref[seqs, h * 128:(h + 1) * 128] = o[h * 8:(h + 1) * 8, :]
-        statbuf[seqs, :] = stat
+            acc_ref[seq8, h * 128:(h + 1) * 128] = o[h * 8:(h + 1) * 8, :]
+        statbuf[seq8, :] = stat
 
     @pl.loop(0, pieces)
     def _(i):
         block_copy(k_hbm, kbuf, k_sem, i).wait()
         block_copy(v_hbm, vbuf, v_sem, i).wait()
-        seqs = piece // BLOCK
 
         @pl.loop(0, seqs, unroll=8)
         def _(j):
-            b = i * seqs + j
-            at = len_smem[b] - base
-            slot = jnp.where(jnp.logical_and(at >= 0, at < BLOCK), b * BLOCK + at, slots)
-            kbuf[slot] = nk[b]
-            vbuf[slot] = nv[b]
-
-        @pl.loop(0, seqs // 8, unroll=2)
+            place_new(i * seqs + j)
+
+        @pl.loop(0, seqs // 8, unroll=UNROLL)
         def _(j):
             attend_tile(i * (seqs // 8) + j)
 
@@ -343,28 +363,27 @@
 def attend(hidden, lengths, k_cache, v_cache, norm_gain, w_query, w_key, w_value):
     batch, block, kv, dim = k_cache.shape
     features, width = w_query.shape
-    slots = batch * block
+    slots = batch * block * kv
     bf16 = lambda *shape: pltpu.VMEM(shape, jnp.bfloat16)
     f32 = lambda *shape: pltpu.VMEM(shape, jnp.float32)
     dma = lambda *shape: pltpu.SemaphoreType.DMA(shape)
-    vmem, hbm = pl.BlockSpec(memory_space=pltpu.VMEM), pl.BlockSpec(memory_space=pl.ANY)
-    cache = jax.ShapeDtypeStruct((slots, kv, dim), jnp.bfloat16)
+    vmem, hbm = pl.BlockSpec(memory_space=pltpu.VMEM), pl.BlockSpec(memory_space=pltpu.HBM)
+    cache = jax.ShapeDtypeStruct((slots, dim), jnp.bfloat16)
     k_new, v_new, acc, stats = pl.pallas_call(
         attend_kernel,
         out_shape=[cache, cache, jax.ShapeDtypeStruct((batch, width), jnp.float32),
                    jax.ShapeDtypeStruct((2 * width // dim, batch), jnp.float32)],
-        in_specs=[pl.BlockSpec(memory_space=pltpu.SMEM), vmem, hbm, vmem, hbm, hbm, hbm, hbm, hbm],
+        in_specs=[pl.BlockSpec(memory_space=pltpu.SMEM), hbm, vmem, hbm, hbm, hbm, hbm, hbm],
         out_specs=[hbm, hbm, vmem, vmem],
         scratch_shapes=[
             bf16(batch, features), bf16(batch, features), bf16(width // 256, features, 256), bf16(features, 256),
-            bf16(features, 256), bf16(slots + 8, kv, dim), bf16(slots + 8, kv, dim), f32(batch, width), f32(2 * batch, dim),
-            bf16(batch, kv, dim), bf16(batch, kv, dim), f32(batch, 128),
+            bf16(features, 256), bf16(slots, dim), bf16(slots, dim), f32(batch, width), f32(kv, batch, dim),
+            f32(kv, batch, dim), f32(batch, 128),
             dma(4), dma(width // 256), pltpu.SemaphoreType.DMA, pltpu.SemaphoreType.DMA, dma(8), dma(8), dma(8), dma(8),
         ],
-        compiler_params=pltpu.CompilerParams(vmem_limit_bytes=60 * 2**20),
+        compiler_params=pltpu.CompilerParams(vmem_limit_bytes=int(ATTEND_VMEM * 2**20)),
         name='attend',
-    )(lengths, jnp.broadcast_to(lengths[:, None], (batch, 128)), hidden, norm_gain.reshape(1, features), w_query, w_key, w_value,
-      k_cache.reshape(slots, kv, dim), v_cache.reshape(slots, kv, dim))
+    )(lengths, hidden, norm_gain, w_query, w_key, w_value, k_cache.reshape(slots, dim), v_cache.reshape(slots, dim))
     return k_new.reshape(k_cache.shape), v_new.reshape(v_cache.shape), acc, stats
 
 

time: 90.2 us -> 84.9 us (0.941)
  local copies, waits for them, and re-layouts: 5.86 us -> 3.13 us
  Pallas kernels: 83.5 us -> 80.9 us
    pallas_call x1, Pallas kernels: 28 us -> 26 us  [attend(): pl.pallas_call(attend_kernel, out_shape=[cache, cache, jax.ShapeDtypeStru...]
    broadcast_in_dim x1 -> x0, local copies, waits for them, and re-layouts: 1.43 us -> none  [attend(): jnp.broadcast_to(lengths[:, None], (batch, 128))]
    reshape x1 -> x0, local copies, waits for them, and re-layouts: 1.3 us -> none  [attend(): norm_gain.reshape(1, features)]
where the time goes in v3:
time: 84.9 us; the launch traced here: 84.7 us
  Pallas kernels  80.9 us (95%)
  local copies, waits for them, and re-layouts  3.13 us (4%)
    pallas_call x1, Pallas kernels, combine(): pl.pallas_call(combine_kernel, out_shape=jax.ShapeDtypeStruct((batch, fea...  54.9 us
    pallas_call x1, Pallas kernels, attend(): pl.pallas_call(attend_kernel, out_shape=[cache, cache, jax.ShapeDtypeStru...  26 us
    unnamed x1, local copies, waits for them, and re-layouts  3.13 us

profile of v3, /device:TPU:0, one launch (start us, length us, event | category | flops | bytes accessed | tf_op | source)
XLA Modules:
  0.0 84.7 jit_solution(12159883234164544436)
XLA Ops:
  0.6 26.0 %attend.1 = (bf16[16384,128]{1,0:T(8,128)(2,1)}, bf16[16384,128]{1,0:T(8,128)(2,1)}, f32[256,1024]{1,0:T(8,128)}, f32[16,256]{1,0:T(8,128)}) custom-call(s32[256]{0:T(256)} %len_ref.1, bf16[256,4096]{1,0:T(8,128)(2,1)} %hid_hbm.3, bf16[4096]{0:T(1024)(128)(2,1)} %gain_ref.1, bf16[4096,1024]{1,0:T(8,128)(2,1)} %wq_hbm.1, bf16[4096,256]{1,0:T(8,128)(2,1)} %wk_hbm.1, ...), custom_call_target="tpu_custom_call" | custom-call | tf_op jit(solution)/shard_map/attend/pallas_call | solution.py:372
  26.6 54.9 %combine.1 = bf16[256,4096]{1,0:T(8,128)(2,1)} custom-call(f32[256,1024]{1,0:T(8,128)} %get-tuple-element.7.acc_ref, f32[16,256]{1,0:T(8,128)} %get-tuple-element.8.stats_ref, bf16[256,4096]{1,0:T(8,128)(2,1)} %hid_hbm.3, bf16[1024,4096]{1,0:T(8,128)(2,1)} %w_hbm.1), custom_call_target="tpu_custom_call" | custom-call | tf_op jit(solution)/shard_map/combine/pallas_call | solution.py:209
  81.5 3.1 %copy.13 = bf16[256,4096]{1,0:T(8,128)(2,1)} copy(bf16[256,4096]{1,0:T(8,128)(2,1)} %combine.1) | data formatting | bytes 4194304

commit v4 on v3

--- a/solution.py
+++ b/solution.py
@@ -10,11 +10,14 @@
 MESH = pl.DeviceIdType.MESH
 HALVES = 2
 COLS = 512
+GROUP = 4
 BLOCK = 32
 SCALE = 128 ** -0.5
-UNROLL = 2
-ATTEND_VMEM = 62.5
-COMBINE_VMEM = 60.5
+UNROLL = 8
+PIECES = 4
+LAGS = (0, 2, 5, 7)
+ATTEND_VMEM = 51.5
+COMBINE_VMEM = 50
 
 
 def combine_kernel(acc_ref, stats_ref, hid_hbm, w_hbm, out_ref, hid_ref, w_ref, stat_in, fac_ref, d2d_in, y_out, y_in, obuf, pbuf,
@@ -125,20 +128,20 @@
     def gs_copy(k, owner):
         return remote(fall.at[owner, k], fall.at[owner, k], gs_s.at[k], gs_r.at[k], sp=sib)
 
-    for r in range(HALVES):
-        if r == 0:
-            w_copy.wait()
-            hid_copy.wait()
+    def merge(r):
         d2d_copies[1][r].wait()
         y_copies[r].wait()
         for j in range(heads):
             obuf[r, :, j * 128:(j + 1) * 128] = (combined(1, r, j) + y_in[r, :, j * 128:(j + 1) * 128]).astype(jnp.bfloat16)
-        for j in range(per_half):
-            k = r * per_half + j
-            pbuf[k] = jnp.dot(obuf[r], w_ref[:, j * COLS:(j + 1) * COLS], preferred_element_type=jnp.float32)
-
-            @pl.when(is_end)
-            def _():
+
+    def project(first):
+        for k in range(first, first + GROUP):
+            cols = slice(k % per_half * COLS, (k % per_half + 1) * COLS)
+            pbuf[k] = jnp.dot(obuf[k // per_half], w_ref[:, cols], preferred_element_type=jnp.float32)
+
+        @pl.when(is_end)
+        def _():
+            for k in range(first, first + GROUP):
                 p_copy(k).start()
 
     def stage_a(k):
@@ -177,11 +180,21 @@
             out_ref[start:start + rows, cols] = (
                 hid_ref[start:start + rows, cols].astype(jnp.float32) + fall[owner, k]).astype(jnp.bfloat16)
 
-    stages = ((stage_a, 0), (stage_f, 2), (stage_y, 4), (stage_o, 6))
-    for step in range(chunks + 6):
+    w_copy.wait()
+    merge(0)
+    for first in range(0, per_half, GROUP):
+        project(first)
+    hid_copy.wait()
+    later = {0: [(merge, 1)]}
+    for i, first in enumerate(range(per_half, chunks, GROUP)):
+        later[1 + i] = [(project, first)]
+    stages = tuple(zip((stage_a, stage_f, stage_y, stage_o), LAGS))
+    for step in range(chunks + LAGS[-1]):
         for stage, lag in stages:
             if 0 <= step - lag < chunks:
                 stage(step - lag)
+        for task, which in later.get(step, ()):
+            task(which)
 
     for k in range(chunks):
         @pl.when(inner)
@@ -232,9 +245,9 @@
     )(acc, stats, hidden, w_out)
 
 
-def attend_kernel(len_ref, hid_hbm, gain_ref, wq_hbm, wk_hbm, wv_hbm, k_hbm, v_hbm, kout_hbm, vout_hbm, acc_ref, stats_ref,
-                  hid, nbuf, wq, wk, wv, kbuf, vbuf, qbuf, nk, nv, statbuf, hid_sem, wq_sem, wk_sem, wv_sem, k_sem, v_sem,
-                  ko_sem, vo_sem):
+def attend_kernel(len_hbm, hid_hbm, gain_hbm, wq_hbm, wk_hbm, wv_hbm, k_hbm, v_hbm, kout_hbm, vout_hbm, acc_ref, stats_ref,
+                  hid, nbuf, wq, wk, wv, kbuf, vbuf, qbuf, nk, nv, statbuf, len_ref, gain_ref, hid_sem, wq_sem, wk_sem, wv_sem, k_sem, v_sem,
+                  ko_sem, vo_sem, len_sem, gain_sem):
     batch, features = hid.shape
     heads = qbuf.shape[1] // 128
     base = lax.axis_index('sp') * BLOCK
@@ -246,33 +259,36 @@
     hid_copies = [copy(hid_hbm.at[pl.ds(i * quarter, quarter), :], hid.at[pl.ds(i * quarter, quarter), :], hid_sem.at[i])
                   for i in range(hid_sem.shape[0])]
     wk_copy, wv_copy = copy(wk_hbm, wk, wk_sem), copy(wv_hbm, wv, wv_sem)
-    wide = wq.shape[2]
-    wq_copies = [copy(wq_hbm.at[:, pl.ds(i * wide, wide)], wq.at[i], wq_sem.at[i]) for i in range(wq.shape[0])]
+    wide, deep = 256, features // wq_sem.shape[0]
+    wq_copies = [copy(wq_hbm.at[pl.ds(i * deep, deep), :], wq.at[pl.ds(i * deep, deep), :], wq_sem.at[i])
+                 for i in range(wq_sem.shape[0])]
 
     def block_copy(src, dst, sem, i):
         rows = pl.ds(pl.multiple_of(i * piece, piece), piece)
         return copy(src.at[rows, :], dst.at[rows, :], sem.at[i])
 
-    for c in hid_copies + [wk_copy, wv_copy]:
+    gain_copy, len_copy = copy(gain_hbm, gain_ref, gain_sem), copy(len_hbm, len_ref, len_sem)
+    for c in [gain_copy, len_copy] + hid_copies + [wk_copy, wv_copy]:
         c.start()
-
-    gain = gain_ref[...].astype(jnp.float32).reshape(1, features)
 
     def norm_rows(i):
         rows = pl.ds(pl.multiple_of(i * 16, 16), 16)
         h = hid[rows, :].astype(jnp.float32)
+        gain = gain_ref[...].astype(jnp.float32).reshape(1, features)
         inv_rms = lax.rsqrt(jnp.mean(h * h, axis=-1, keepdims=True) + EPS)
         nbuf[rows, :] = (h * inv_rms * gain).astype(jnp.bfloat16)
 
     for i, c in enumerate(hid_copies):
         c.wait()
         if i == 0:
-            for w in wq_copies:
-                w.start()
-        if i == 1:
+            gain_copy.wait()
+            len_copy.wait()
             for j in range(pieces):
                 block_copy(k_hbm, kbuf, k_sem, j).start()
                 block_copy(v_hbm, vbuf, v_sem, j).start()
+        if i == 2:
+            for w in wq_copies:
+                w.start()
         per = quarter // 16
         pl.loop(i * per, (i + 1) * per)(norm_rows)
 
@@ -282,11 +298,6 @@
         new = new.astype(jnp.bfloat16).astype(jnp.float32)
         for j in range(2):
             out[j] = new[:, j * 128:(j + 1) * 128]
-
-    for i, c in enumerate(wq_copies):
-        c.wait()
-        query = jnp.dot(nbuf[...], wq[i], preferred_element_type=jnp.float32)
-        qbuf[:, i * wide:(i + 1) * wide] = query.astype(jnp.bfloat16).astype(jnp.float32)
 
     lane = lax.broadcasted_iota(jnp.int32, (8, 128), 1)
     row = lax.broadcasted_iota(jnp.int32, (8, 128), 0)
@@ -297,60 +308,90 @@
     odd_row = row % 2 == 1
     slot_row = lax.broadcasted_iota(jnp.int32, (16, 128), 0) // 2
 
-    def place_new(b):
-        at = len_ref[b] - base
-        first = jnp.clip(at, 0, BLOCK - 1) // 8
-        rows = pl.ds(pl.multiple_of(b * 2 * BLOCK + first * 16, 16), 16)
-        here = slot_row == at - first * 8
-        for buf, new in ((kbuf, nk), (vbuf, nv)):
-            fresh = jnp.where(odd_row, jnp.broadcast_to(new[1, pl.ds(b, 1), :], (8, 128)),
-                              jnp.broadcast_to(new[0, pl.ds(b, 1), :], (8, 128)))
-            fresh = jnp.concatenate([fresh, fresh], axis=0)
-            buf[rows, :] = jnp.where(here, fresh, buf[rows, :].astype(jnp.float32)).astype(jnp.bfloat16)
-
-    def attend_tile(i):
+    def place_new(g):
+        group = pl.ds(pl.multiple_of(g * 8, 8), 8)
+        news = [(new[0, group, :], new[1, group, :]) for new in (nk, nv)]
+        spots = []
+        for j in range(8):
+            b = g * 8 + j
+            at = len_ref[b] - base
+            first = jnp.clip(at, 0, BLOCK - 1) // 8
+            rows = pl.ds(pl.multiple_of(b * 2 * BLOCK + first * 16, 16), 16)
+            spots.append((rows, slot_row == at - first * 8))
+        olds = [(kbuf[rows, :], vbuf[rows, :]) for rows, _ in spots]
+        for j, (rows, here) in enumerate(spots):
+            for buf, (low, high), old in zip((kbuf, vbuf), news, olds[j]):
+                fresh = jnp.where(odd_row, jnp.broadcast_to(high[j:j + 1], (8, 128)), jnp.broadcast_to(low[j:j + 1], (8, 128)))
+                fresh = jnp.concatenate([fresh, fresh], axis=0)
+                buf[rows, :] = jnp.where(here, fresh, old.astype(jnp.float32)).astype(jnp.bfloat16)
+
+    def scores(i):
         seq8 = pl.ds(pl.multiple_of(i * 8, 8), 8)
         keys = pl.ds(pl.multiple_of(i * 512, 512), 512)
         q = jnp.concatenate([qbuf[seq8, h * 128:(h + 1) * 128] for h in range(heads)], axis=0).astype(jnp.bfloat16)
         s = lax.dot_general(q, kbuf[keys, :], (((1,), (1,)), ((), ())), preferred_element_type=jnp.float32)
+        out = []
+        for h in range(heads):
+            part = [s[h * 8:(h + 1) * 8, j * 128:(j + 1) * 128] for j in range(4)]
+            out.append(jnp.where(pairs[0], part[0], jnp.where(pairs[1], part[1], jnp.where(pairs[2], part[2], part[3]))))
+        return out
+
+    def softmax(i, score_list):
+        seq8 = pl.ds(pl.multiple_of(i * 8, 8), 8)
         lens = jnp.full((8, 128), len_ref[i * 8], jnp.int32)
         for j in range(1, 8):
             lens = jnp.where(row == j, len_ref[i * 8 + j], lens)
         valid = jnp.logical_and(own_seq, slot_pos <= lens)
         valids = (jnp.logical_and(valid, even), jnp.logical_and(valid, jnp.logical_not(even)))
+        oks = [valids[h // (heads // 2)] for h in range(heads)]
+        masked = [jnp.where(ok, score * SCALE, NEG_BIG) for ok, score in zip(oks, score_list)]
+        peaks = [jnp.max(score, axis=1, keepdims=True) for score in masked]
+        exps = [jnp.where(ok, jnp.exp(score - peak), 0.0) for ok, score, peak in zip(oks, masked, peaks)]
+        sums = [jnp.sum(e, axis=1, keepdims=True) for e in exps]
         stat = jnp.zeros((8, 128), jnp.float32)
-        probs = []
         for h in range(heads):
-            part = [s[h * 8:(h + 1) * 8, j * 128:(j + 1) * 128] for j in range(4)]
-            score = jnp.where(pairs[0], part[0], jnp.where(pairs[1], part[1], jnp.where(pairs[2], part[2], part[3])))
-            ok = valids[h // (heads // 2)]
-            score = jnp.where(ok, score * SCALE, NEG_BIG)
-            peak = jnp.max(score, axis=1, keepdims=True)
-            e = jnp.where(ok, jnp.exp(score - peak), 0.0)
-            stat = jnp.where(lane == h, peak, stat)
-            stat = jnp.where(lane == heads + h, jnp.sum(e, axis=1, keepdims=True), stat)
-            probs.append(jnp.concatenate([jnp.where(pairs[j], e, 0.0) for j in range(4)], axis=1))
-        p = jnp.concatenate(probs, axis=0).astype(jnp.bfloat16)
+            stat = jnp.where(lane == h, peaks[h], jnp.where(lane == heads + h, sums[h], stat))
+        statbuf[seq8, :] = stat
+        probs = [jnp.concatenate([jnp.where(pairs[j], e, 0.0) for j in range(4)], axis=1) for e in exps]
+        return jnp.concatenate(probs, axis=0).astype(jnp.bfloat16)
+
+    def values(i, p):
+        seq8 = pl.ds(pl.multiple_of(i * 8, 8), 8)
+        keys = pl.ds(pl.multiple_of(i * 512, 512), 512)
         o = jnp.dot(p, vbuf[keys, :], preferred_element_type=jnp.float32)
         for h in range(heads):
             acc_ref[seq8, h * 128:(h + 1) * 128] = o[h * 8:(h + 1) * 8, :]
-        statbuf[seq8, :] = stat
+
+    per_piece = seqs // 8
 
     @pl.loop(0, pieces)
     def _(i):
         block_copy(k_hbm, kbuf, k_sem, i).wait()
         block_copy(v_hbm, vbuf, v_sem, i).wait()
 
-        @pl.loop(0, seqs, unroll=8)
+        @pl.loop(0, per_piece)
         def _(j):
-            place_new(i * seqs + j)
-
-        @pl.loop(0, seqs // 8, unroll=UNROLL)
-        def _(j):
-            attend_tile(i * (seqs // 8) + j)
-
+            place_new(i * per_piece + j)
+
+    for c in wq_copies:
+        c.wait()
+    for i in range(wq.shape[1] // wide):
+        query = jnp.dot(nbuf[...], wq[:, i * wide:(i + 1) * wide], preferred_element_type=jnp.float32)
+        qbuf[:, i * wide:(i + 1) * wide] = query.astype(jnp.bfloat16).astype(jnp.float32)
+
+    for i in range(pieces):
         block_copy(kbuf, kout_hbm, ko_sem, i).start()
         block_copy(vbuf, vout_hbm, vo_sem, i).start()
+
+    @pl.loop(0, pieces)
+    def _(i):
+        @pl.loop(0, per_piece, step=UNROLL)
+        def _(j):
+            tiles = [i * per_piece + j + u for u in range(UNROLL)]
+            score_lists = [scores(t) for t in tiles]
+            prob_list = [softmax(t, score_list) for t, score_list in zip(tiles, score_lists)]
+            for t, p in zip(tiles, prob_list):
+                values(t, p)
 
     for i in range(batch // 128):
         stats_ref[:, i * 128:(i + 1) * 128] = statbuf[i * 128:(i + 1) * 128, :].T[0:2 * heads, :]
@@ -366,20 +407,20 @@
     slots = batch * block * kv
     bf16 = lambda *shape: pltpu.VMEM(shape, jnp.bfloat16)
     f32 = lambda *shape: pltpu.VMEM(shape, jnp.float32)
-    dma = lambda *shape: pltpu.SemaphoreType.DMA(shape)
-    vmem, hbm = pl.BlockSpec(memory_space=pltpu.VMEM), pl.BlockSpec(memory_space=pltpu.HBM)
+    dma, one = lambda *shape: pltpu.SemaphoreType.DMA(shape), pltpu.SemaphoreType.DMA
+    hbm, vmem = pl.BlockSpec(memory_space=pltpu.HBM), pl.BlockSpec(memory_space=pltpu.VMEM)
     cache = jax.ShapeDtypeStruct((slots, dim), jnp.bfloat16)
     k_new, v_new, acc, stats = pl.pallas_call(
         attend_kernel,
         out_shape=[cache, cache, jax.ShapeDtypeStruct((batch, width), jnp.float32),
                    jax.ShapeDtypeStruct((2 * width // dim, batch), jnp.float32)],
-        in_specs=[pl.BlockSpec(memory_space=pltpu.SMEM), hbm, vmem, hbm, hbm, hbm, hbm, hbm],
+        in_specs=[hbm] * 8,
         out_specs=[hbm, hbm, vmem, vmem],
         scratch_shapes=[
-            bf16(batch, features), bf16(batch, features), bf16(width // 256, features, 256), bf16(features, 256),
+            bf16(batch, features), bf16(batch, features), bf16(features, width), bf16(features, 256),
             bf16(features, 256), bf16(slots, dim), bf16(slots, dim), f32(batch, width), f32(kv, batch, dim),
-            f32(kv, batch, dim), f32(batch, 128),
-            dma(4), dma(width // 256), pltpu.SemaphoreType.DMA, pltpu.SemaphoreType.DMA, dma(8), dma(8), dma(8), dma(8),
+            f32(kv, batch, dim), f32(batch, 128), pltpu.SMEM((batch,), jnp.int32), bf16(features),
+            dma(4), dma(width // 256), one, one, dma(PIECES), dma(PIECES), dma(PIECES), dma(PIECES), one, one,
         ],
         compiler_params=pltpu.CompilerParams(vmem_limit_bytes=int(ATTEND_VMEM * 2**20)),
         name='attend',

time: 84.9 us -> 68.1 us (0.80)
  Pallas kernels: 80.9 us -> 64.5 us
    pallas_call x1, Pallas kernels: 26 us -> 13.9 us  [attend(): pl.pallas_call(attend_kernel, out_shape=[cache, cache, jax.ShapeDtypeStru...]
    pallas_call x1, Pallas kernels: 54.9 us -> 50.7 us  [combine(): pl.pallas_call(combine_kernel, out_shape=jax.ShapeDtypeStruct((batch, fea...]
    unnamed x1 -> x5, local copies, waits for them, and re-layouts: 3.13 us -> 2.69 us
where the time goes in v4:
time: 68.1 us; the launch traced here: 67.9 us
  Pallas kernels  64.5 us (95%)
  local copies, waits for them, and re-layouts  2.69 us (4%)
    pallas_call x1, Pallas kernels, combine(): pl.pallas_call(combine_kernel, out_shape=jax.ShapeDtypeStruct((batch, fea...  50.7 us
    pallas_call x1, Pallas kernels, attend(): pl.pallas_call(attend_kernel, out_shape=[cache, cache, jax.ShapeDtypeStru...  13.9 us
    unnamed x5, local copies, waits for them, and re-layouts  2.69 us

profile of v4, /device:TPU:0, one launch (start us, length us, event | category | flops | bytes accessed | tf_op | source)
XLA Modules:
  0.0 67.9 jit_solution(9795183807447144939)
XLA Ops:
  0.6 0.0 copy-start
  0.6 0.7 %copy-done = bf16[4096]{0:T(1024)(128)(2,1)S(1)} copy-done((bf16[4096]{0:T(1024)(128)(2,1)S(1)}, bf16[4096]{0:T(1024)(128)(2,1)}, u32[]{:S(2)}) %copy-start) | copy-done | bytes 8216
  1.3 0.0 copy-start.1
  1.3 0.7 copy-done.1
  2.0 13.9 %attend.1 = (bf16[16384,128]{1,0:T(8,128)(2,1)}, bf16[16384,128]{1,0:T(8,128)(2,1)}, f32[256,1024]{1,0:T(8,128)S(1)}, f32[16,256]{1,0:T(8,128)S(1)}) custom-call(s32[256]{0:T(256)S(1)} %copy-done.1, bf16[256,4096]{1,0:T(8,128)(2,1)} %hid_hbm.3, bf16[4096]{0:T(1024)(128)(2,1)S(1)} %copy-done, bf16[4096,1024]{1,0:T(8,128)(2,1)} %wq_hbm.1, ...), custom_call_target="tpu_custom_call" | custom-call | tf_op jit(solution)/shard_map/attend/pallas_call | solution.py:413
  15.9 50.7 %combine.1 = bf16[256,4096]{1,0:T(8,128)(2,1)S(1)} custom-call(f32[256,1024]{1,0:T(8,128)S(1)} %get-tuple-element.7.acc_ref, f32[16,256]{1,0:T(8,128)S(1)} %get-tuple-element.8.stats_ref, bf16[256,4096]{1,0:T(8,128)(2,1)} %hid_hbm.3, bf16[1024,4096]{1,0:T(8,128)(2,1)} %w_hbm.1), custom_call_target="tpu_custom_call" | custom-call | tf_op jit(solution)/shard_map/combine/pallas_call | solution.py:222
  66.5 1.3 %copy.13 = bf16[256,4096]{1,0:T(8,128)(2,1)} copy(bf16[256,4096]{1,0:T(8,128)(2,1)S(1)} %combine.1) | data formatting | bytes 4194304
Async XLA Ops:
  0.6 0.7 %copy-start = (bf16[4096]{0:T(1024)(128)(2,1)S(1)}, bf16[4096]{0:T(1024)(128)(2,1)}, u32[]{:S(2)}) copy-start(bf16[4096]{0:T(1024)(128)(2,1)} %gain_hbm.1) | copy-start | bytes 24580
  1.3 0.7 %copy-start.1 = (s32[256]{0:T(256)S(1)}, s32[256]{0:T(256)}, u32[]{:S(2)}) copy-start(s32[256]{0:T(256)} %len_hbm.1) | copy-start | bytes 3076

commit v5 on v4

--- a/solution.py
+++ b/solution.py
@@ -8,14 +8,15 @@
 EPS = 1e-6
 NEG_BIG = -1e30
 MESH = pl.DeviceIdType.MESH
-HALVES = 2
-COLS = 512
+HALVES = 4
+EARLY = 2
+COLS = 1024
 GROUP = 4
 BLOCK = 32
 SCALE = 128 ** -0.5
 UNROLL = 8
 PIECES = 4
-LAGS = (0, 2, 5, 7)
+LAGS = (0, 3, 6, 8)
 ATTEND_VMEM = 51.5
 COMBINE_VMEM = 50
 
@@ -76,29 +77,25 @@
         return remote(acc_ref.at[pl.ds(start, rows), :], d2d_in.at[t, r], dd_s.at[2 * r + t], dd_r.at[2 * r + t], sp=sib)
 
     d2d_copies = [[d2d_copy(t, r) for r in range(HALVES)] for t in range(2)]
-    for r in range(HALVES):
-        for t in range(2):
+    for t in range(2):
+        for r in range(HALVES):
             d2d_copies[t][r].start()
 
-    for copy in stat_copies:
-        copy.wait()
     lanes = pl.ds(pl.multiple_of(c * 2 * own_rows, 128), 2 * own_rows)
-    peaks = [stats_ref[0:heads, lanes]] + [stat_in[i, 0:heads, :] for i in range(3)]
-    sums = [stats_ref[heads:2 * heads, lanes]] + [stat_in[i, heads:2 * heads, :] for i in range(3)]
-    top = jnp.maximum(jnp.maximum(peaks[0], peaks[1]), jnp.maximum(peaks[2], peaks[3]))
-    weights = [jnp.exp(peak - top) for peak in peaks]
-    total = sums[0] * weights[0] + sums[1] * weights[1] + (sums[2] * weights[2] + sums[3] * weights[3])
-    factors = jnp.concatenate(
-        [weights[0] / total, weights[1] / total, jnp.zeros((2 * own_rows - 2 * heads, 2 * own_rows), jnp.float32)], axis=0)
-    fac_ref[...] = factors.T
+    stat_copies[0].wait()
+    peaks = [stats_ref[0:heads, lanes], stat_in[0, 0:heads, :]]
+    sums = [stats_ref[heads:2 * heads, lanes], stat_in[0, heads:2 * heads, :]]
+    chip_top = jnp.maximum(peaks[0], peaks[1])
+    unused = jnp.zeros((2 * own_rows - 2 * heads, 2 * own_rows), jnp.float32)
+    fac_ref[0] = jnp.concatenate([jnp.exp(peaks[0] - chip_top), jnp.exp(peaks[1] - chip_top), unused], axis=0).T
 
     def combined(t, r, j):
         plane = (1 - y) if t == 0 else y
         base = pl.multiple_of(plane * own_rows + r * rows, rows)
         start = pl.multiple_of(c * 2 * own_rows + base, rows)
         cols = slice(j * 128, (j + 1) * 128)
-        mine = acc_ref[pl.ds(start, rows), cols] * fac_ref[pl.ds(base, rows), j:j + 1]
-        return mine + d2d_in[t, r, :, cols] * fac_ref[pl.ds(base, rows), heads + j:heads + j + 1]
+        mine = acc_ref[pl.ds(start, rows), cols] * fac_ref[0, pl.ds(base, rows), j:j + 1]
+        return mine + d2d_in[t, r, :, cols] * fac_ref[0, pl.ds(base, rows), heads + j:heads + j + 1]
 
     def y_copy(r):
         return remote(y_out.at[r], y_in.at[r], yy_s.at[r], yy_r.at[r], sp=yn)
@@ -110,6 +107,16 @@
             y_out[r, :, j * 128:(j + 1) * 128] = combined(0, r, j)
         y_copies[r].start()
 
+    for copy in stat_copies[1:]:
+        copy.wait()
+    peaks += [stat_in[i, 0:heads, :] for i in (1, 2)]
+    sums += [stat_in[i, heads:2 * heads, :] for i in (1, 2)]
+    far_top = jnp.maximum(peaks[2], peaks[3])
+    top = jnp.maximum(chip_top, far_top)
+    parts = [one_sum * jnp.exp(peak - top) for one_sum, peak in zip(sums, peaks)]
+    total = parts[0] + parts[1] + (parts[2] + parts[3])
+    fac_ref[1] = jnp.concatenate([jnp.exp(chip_top - top) / total, jnp.exp(far_top - top) / total, unused], axis=0).T
+
     def p_copy(k):
         return remote(pbuf.at[k], pe_in.at[k], p_s.at[k], p_r.at[k], tp=inner_z)
 
@@ -131,8 +138,11 @@
     def merge(r):
         d2d_copies[1][r].wait()
         y_copies[r].wait()
+        base = pl.multiple_of(y * own_rows + r * rows, rows)
         for j in range(heads):
-            obuf[r, :, j * 128:(j + 1) * 128] = (combined(1, r, j) + y_in[r, :, j * 128:(j + 1) * 128]).astype(jnp.bfloat16)
+            near = combined(1, r, j) * fac_ref[1, pl.ds(base, rows), j:j + 1]
+            far = y_in[r, :, j * 128:(j + 1) * 128] * fac_ref[1, pl.ds(base, rows), heads + j:heads + j + 1]
+            obuf[r, :, j * 128:(j + 1) * 128] = (near + far).astype(jnp.bfloat16)
 
     def project(first):
         for k in range(first, first + GROUP):
@@ -181,13 +191,16 @@
                 hid_ref[start:start + rows, cols].astype(jnp.float32) + fall[owner, k]).astype(jnp.bfloat16)
 
     w_copy.wait()
-    merge(0)
-    for first in range(0, per_half, GROUP):
-        project(first)
+    for r in range(EARLY):
+        merge(r)
+        for first in range(r * per_half, (r + 1) * per_half, GROUP):
+            project(first)
     hid_copy.wait()
-    later = {0: [(merge, 1)]}
-    for i, first in enumerate(range(per_half, chunks, GROUP)):
-        later[1 + i] = [(project, first)]
+    later = {}
+    for r in range(EARLY, HALVES):
+        later.setdefault(r - EARLY, []).append((merge, r))
+        for i, first in enumerate(range(r * per_half, (r + 1) * per_half, GROUP)):
+            later.setdefault(r - EARLY + i + (HALVES == 2), []).append((project, first))
     stages = tuple(zip((stage_a, stage_f, stage_y, stage_o), LAGS))
     for step in range(chunks + LAGS[-1]):
         for stage, lag in stages:
@@ -228,7 +241,7 @@
             pltpu.VMEM(hidden.shape, jnp.bfloat16),
             pltpu.VMEM(w_out.shape, jnp.bfloat16),
             f32(3, stats.shape[0], batch // 2),
-            f32(batch // 2, batch // 2),
+            f32(2, batch // 2, batch // 2),
             f32(2, HALVES, rows, width),
             f32(HALVES, rows, width),
             f32(HALVES, rows, width),

time: 68.1 us -> 65.6 us (0.963)
  Pallas kernels: 64.5 us -> 62.1 us
    pallas_call x1, Pallas kernels: 50.7 us -> 48.2 us  [combine(): pl.pallas_call(combine_kernel, out_shape=jax.ShapeDtypeStruct((batch, fea...]
where the time goes in v5:
time: 65.6 us; the launch traced here: 65.4 us
  Pallas kernels  62.1 us (95%)
  local copies, waits for them, and re-layouts  2.69 us (4%)
  between operations  0.66 us (1%)
    pallas_call x1, Pallas kernels, combine(): pl.pallas_call(combine_kernel, out_shape=jax.ShapeDtypeStruct((batch, fea...  48.2 us
    pallas_call x1, Pallas kernels, attend(): pl.pallas_call(attend_kernel, out_shape=[cache, cache, jax.ShapeDtypeStru...  13.9 us
    unnamed x5, local copies, waits for them, and re-layouts  2.69 us

profile of v5, /device:TPU:0, one launch (start us, length us, event | category | flops | bytes accessed | tf_op | source)
XLA Modules:
  0.0 65.4 jit_solution(8931976585917558772)
XLA Ops:
  0.6 0.0 copy-start
  0.6 0.7 %copy-done = bf16[4096]{0:T(1024)(128)(2,1)S(1)} copy-done((bf16[4096]{0:T(1024)(128)(2,1)S(1)}, bf16[4096]{0:T(1024)(128)(2,1)}, u32[]{:S(2)}) %copy-start) | copy-done | bytes 8216
  1.3 0.0 copy-start.1
  1.3 0.7 %copy-done.1 = s32[256]{0:T(256)S(1)} copy-done((s32[256]{0:T(256)S(1)}, s32[256]{0:T(256)}, u32[]{:S(2)}) %copy-start.1) | copy-done | bytes 1048
  2.0 13.9 %attend.1 = (bf16[16384,128]{1,0:T(8,128)(2,1)}, bf16[16384,128]{1,0:T(8,128)(2,1)}, f32[256,1024]{1,0:T(8,128)S(1)}, f32[16,256]{1,0:T(8,128)S(1)}) custom-call(s32[256]{0:T(256)S(1)} %copy-done.1, bf16[256,4096]{1,0:T(8,128)(2,1)} %hid_hbm.3, bf16[4096]{0:T(1024)(128)(2,1)S(1)} %copy-done, bf16[4096,1024]{1,0:T(8,128)(2,1)} %wq_hbm.1, ...), custom_call_target="tpu_custom_call" | custom-call | tf_op jit(solution)/shard_map/attend/pallas_call | solution.py:426
  15.9 48.2 %combine.1 = bf16[256,4096]{1,0:T(8,128)(2,1)S(1)} custom-call(f32[256,1024]{1,0:T(8,128)S(1)} %get-tuple-element.7.acc_ref, f32[16,256]{1,0:T(8,128)S(1)} %get-tuple-element.8.stats_ref, bf16[256,4096]{1,0:T(8,128)(2,1)} %hid_hbm.3, bf16[1024,4096]{1,0:T(8,128)(2,1)} %w_hbm.1), custom_call_target="tpu_custom_call" | custom-call | tf_op jit(solution)/shard_map/combine/pallas_call | solution.py:235
  64.1 1.3 %copy.13 = bf16[256,4096]{1,0:T(8,128)(2,1)} copy(bf16[256,4096]{1,0:T(8,128)(2,1)S(1)} %combine.1) | data formatting | bytes 4194304
Async XLA Ops:
  0.6 0.7 %copy-start = (bf16[4096]{0:T(1024)(128)(2,1)S(1)}, bf16[4096]{0:T(1024)(128)(2,1)}, u32[]{:S(2)}) copy-start(bf16[4096]{0:T(1024)(128)(2,1)} %gain_hbm.1) | copy-start | bytes 24580
  1.3 0.7 %copy-start.1 = (s32[256]{0:T(256)S(1)}, s32[256]{0:T(256)}, u32[]{:S(2)}) copy-start(s32[256]{0:T(256)} %len_hbm.1) | copy-start | bytes 3076

commit v6 on v5

--- a/solution.py
+++ b/solution.py
@@ -118,22 +118,22 @@
     fac_ref[1] = jnp.concatenate([jnp.exp(chip_top - top) / total, jnp.exp(far_top - top) / total, unused], axis=0).T
 
     def p_copy(k):
-        return remote(pbuf.at[k], pe_in.at[k], p_s.at[k], p_r.at[k], tp=inner_z)
+        return remote(pbuf.at[k], pe_in.at[k], p_s, p_r.at[k], tp=inner_z)
 
     def a_copy(k):
-        return remote(abuf.at[k], mb_in.at[k], a_s.at[k], a_r.at[k], tp=mid_z)
+        return remote(abuf.at[k], mb_in.at[k], a_s, a_r.at[k], tp=mid_z)
 
     def fz_copy(k):
-        return remote(fall.at[sp, k], fall.at[sp, k], fz_s.at[k], fz_r.at[k], tp=end_z)
+        return remote(fall.at[sp, k], fall.at[sp, k], fz_s, fz_r.at[k], tp=end_z)
 
     def fy_copy(k, owner):
-        return remote(fall.at[owner, k], fall.at[owner, k], fy_s.at[k], fy_r.at[k], sp=yn)
+        return remote(fall.at[owner, k], fall.at[owner, k], fy_s, fy_r.at[k], sp=yn)
 
     def fs_copy(k, owner):
-        return remote(fall.at[owner, k], fall.at[owner, k], fs_s.at[k], fs_r.at[k], sp=sib)
+        return remote(fall.at[owner, k], fall.at[owner, k], fs_s, fs_r.at[k], sp=sib)
 
     def gs_copy(k, owner):
-        return remote(fall.at[owner, k], fall.at[owner, k], gs_s.at[k], gs_r.at[k], sp=sib)
+        return remote(fall.at[owner, k], fall.at[owner, k], gs_s, gs_r.at[k], sp=sib)
 
     def merge(r):
         d2d_copies[1][r].wait()
@@ -209,19 +209,21 @@
         for task, which in later.get(step, ()):
             task(which)
 
-    for k in range(chunks):
-        @pl.when(inner)
-        def _():
-            a_copy(k).wait_send()
-            fz_copy(k).wait_send()
-
-        @pl.when(is_end)
-        def _():
-            p_copy(k).wait_send()
-
-        fy_copy(k, sp).wait_send()
-        fs_copy(k, sp).wait_send()
-        gs_copy(k, yn).wait_send()
+    def all_sent(src, send, **where):
+        remote(src, src, send, fs_r.at[0], **where).wait_send()
+
+    @pl.when(inner)
+    def _():
+        all_sent(abuf, a_s, tp=mid_z)
+        all_sent(fall.at[sp], fz_s, tp=end_z)
+
+    @pl.when(is_end)
+    def _():
+        all_sent(pbuf, p_s, tp=inner_z)
+
+    all_sent(fall.at[sp], fy_s, sp=yn)
+    all_sent(fall.at[sp], fs_s, sp=sib)
+    all_sent(fall.at[yn], gs_s, sp=sib)
 
 
 def combine(acc, stats, hidden, w_out):
@@ -252,7 +254,7 @@
             f32(chunks, rows, COLS),
             f32(4, chunks, rows, COLS),
             pltpu.SemaphoreType.DMA, pltpu.SemaphoreType.DMA, dma(3), dma(3), dma(2 * HALVES), dma(2 * HALVES), dma(HALVES), dma(HALVES),
-        ] + [dma(chunks)] * 12,
+        ] + [pltpu.SemaphoreType.DMA, dma(chunks)] * 6,
         compiler_params=pltpu.CompilerParams(collective_id=0, has_side_effects=True, vmem_limit_bytes=int(COMBINE_VMEM * 2**20)),
         name='combine',
     )(acc, stats, hidden, w_out)
@@ -437,7 +439,7 @@
         ],
         compiler_params=pltpu.CompilerParams(vmem_limit_bytes=int(ATTEND_VMEM * 2**20)),
         name='attend',
-    )(lengths, hidden, norm_gain, w_query, w_key, w_value, k_cache.reshape(slots, dim), v_cache.reshape(slots, dim))
+    )(pltpu.with_memory_space_constraint(lengths, pltpu.HBM), hidden, pltpu.with_memory_space_constraint(norm_gain, pltpu.HBM), w_query, w_key, w_value, k_cache.reshape(slots, dim), v_cache.reshape(slots, dim))
     return k_new.reshape(k_cache.shape), v_new.reshape(v_cache.shape), acc, stats
 
 

time: 65.6 us -> 63.5 us (0.968)
  local copies, waits for them, and re-layouts: 2.69 us -> 1.32 us
  Pallas kernels: 62.1 us -> 61.4 us
    unnamed x5 -> x1, local copies, waits for them, and re-layouts: 2.69 us -> 1.32 us
    pallas_call x1, Pallas kernels: 48.2 us -> 47.4 us  [combine(): pl.pallas_call(combine_kernel, out_shape=jax.ShapeDtypeStruct((batch, fea...]
where the time goes in v6:
time: 63.5 us; the launch traced here: 63.4 us
  Pallas kernels  61.4 us (97%)
  local copies, waits for them, and re-layouts  1.32 us (2%)
  between operations  0.65 us (1%)
    pallas_call x1, Pallas kernels, combine(): pl.pallas_call(combine_kernel, out_shape=jax.ShapeDtypeStruct((batch, fea...  47.4 us
    pallas_call x1, Pallas kernels, attend(): pl.pallas_call(attend_kernel, out_shape=[cache, cache, jax.ShapeDtypeStru...  14 us
    unnamed x1, local copies, waits for them, and re-layouts  1.32 us

profile of v6, /device:TPU:0, one launch (start us, length us, event | category | flops | bytes accessed | tf_op | source)
XLA Modules:
  0.0 63.4 jit_solution(11099647508558398510)
XLA Ops:
  0.6 14.0 %attend.1 = (bf16[16384,128]{1,0:T(8,128)(2,1)}, bf16[16384,128]{1,0:T(8,128)(2,1)}, f32[256,1024]{1,0:T(8,128)S(1)}, f32[16,256]{1,0:T(8,128)S(1)}) custom-call(s32[256]{0:T(256)} %len_hbm.1, bf16[256,4096]{1,0:T(8,128)(2,1)} %hid_hbm.3, bf16[4096]{0:T(1024)(128)(2,1)} %gain_hbm.1, bf16[4096,1024]{1,0:T(8,128)(2,1)} %wq_hbm.1, bf16[4096,256]{1,0:T(8,128)(2,1)} %wk_hbm.1, ...), custom_call_target="tpu_custom_call" | custom-call | tf_op jit(solution)/shard_map/attend/pallas_call | solution.py:428
  14.6 47.4 %combine.1 = bf16[256,4096]{1,0:T(8,128)(2,1)S(1)} custom-call(f32[256,1024]{1,0:T(8,128)S(1)} %get-tuple-element.7.acc_ref, f32[16,256]{1,0:T(8,128)S(1)} %get-tuple-element.8.stats_ref, bf16[256,4096]{1,0:T(8,128)(2,1)} %hid_hbm.3, bf16[1024,4096]{1,0:T(8,128)(2,1)} %w_hbm.1), custom_call_target="tpu_custom_call" | custom-call | tf_op jit(solution)/shard_map/combine/pallas_call | solution.py:237
  62.0 1.3 %copy.13 = bf16[256,4096]{1,0:T(8,128)(2,1)} copy(bf16[256,4096]{1,0:T(8,128)(2,1)S(1)} %combine.1) | data formatting | bytes 4194304

commit v7 on v6

--- a/solution.py
+++ b/solution.py
@@ -9,13 +9,13 @@
 NEG_BIG = -1e30
 MESH = pl.DeviceIdType.MESH
 HALVES = 4
-EARLY = 2
+EARLY = 1
 COLS = 1024
 GROUP = 4
 BLOCK = 32
 SCALE = 128 ** -0.5
-UNROLL = 8
-PIECES = 4
+UNROLL = 16
+PIECES = 2
 LAGS = (0, 3, 6, 8)
 ATTEND_VMEM = 51.5
 COMBINE_VMEM = 50

time: 63.5 us -> 62.7 us (0.987)
  Pallas kernels: 61.4 us -> 60.6 us
    pallas_call x1, Pallas kernels: 14 us -> 13.2 us  [attend(): pl.pallas_call(attend_kernel, out_shape=[cache, cache, jax.ShapeDtypeStru...]
where the time goes in v7:
time: 62.7 us; the launch traced here: 62.5 us
  Pallas kernels  60.6 us (97%)
  local copies, waits for them, and re-layouts  1.32 us (2%)
  between operations  0.65 us (1%)
    pallas_call x1, Pallas kernels, combine(): pl.pallas_call(combine_kernel, out_shape=jax.ShapeDtypeStruct((batch, fea...  47.4 us
    pallas_call x1, Pallas kernels, attend(): pl.pallas_call(attend_kernel, out_shape=[cache, cache, jax.ShapeDtypeStru...  13.2 us
    unnamed x1, local copies, waits for them, and re-layouts  1.32 us

profile of v7, /device:TPU:0, one launch (start us, length us, event | category | flops | bytes accessed | tf_op | source)
XLA Modules:
  0.0 62.5 jit_solution(7562826017426389720)
XLA Ops:
  0.6 13.2 %attend.1 = (bf16[16384,128]{1,0:T(8,128)(2,1)}, bf16[16384,128]{1,0:T(8,128)(2,1)}, f32[256,1024]{1,0:T(8,128)S(1)}, f32[16,256]{1,0:T(8,128)S(1)}) custom-call(s32[256]{0:T(256)} %len_hbm.1, bf16[256,4096]{1,0:T(8,128)(2,1)} %hid_hbm.3, bf16[4096]{0:T(1024)(128)(2,1)} %gain_hbm.1, bf16[4096,1024]{1,0:T(8,128)(2,1)} %wq_hbm.1, bf16[4096,256]{1,0:T(8,128)(2,1)} %wk_hbm.1, ...), custom_call_target="tpu_custom_call" | custom-call | tf_op jit(solution)/shard_map/attend/pallas_call | solution.py:428
  13.8 47.4 %combine.1 = bf16[256,4096]{1,0:T(8,128)(2,1)S(1)} custom-call(f32[256,1024]{1,0:T(8,128)S(1)} %get-tuple-element.7.acc_ref, f32[16,256]{1,0:T(8,128)S(1)} %get-tuple-element.8.stats_ref, bf16[256,4096]{1,0:T(8,128)(2,1)} %hid_hbm.3, bf16[1024,4096]{1,0:T(8,128)(2,1)} %w_hbm.1), custom_call_target="tpu_custom_call" | custom-call | tf_op jit(solution)/shard_map/combine/pallas_call | solution.py:237
  61.2 1.3 %copy.13 = bf16[256,4096]{1,0:T(8,128)(2,1)} copy(bf16[256,4096]{1,0:T(8,128)(2,1)S(1)} %combine.1) | data formatting | bytes 4194304

commit v8 on v7

--- a/solution.py
+++ b/solution.py
@@ -65,7 +65,7 @@
 
     def stat_copy(i, peer):
         lanes = pl.ds(pl.multiple_of((peer % 2) * 2 * own_rows, 128), 2 * own_rows)
-        return remote(stats_ref.at[:, lanes], stat_in.at[i], st_s.at[i], st_r.at[i], sp=peer)
+        return remote(stats_ref.at[:, lanes], stat_in.at[i], st_s, st_r.at[i], sp=peer)
 
     stat_copies = [stat_copy(i, peer) for i, peer in enumerate((sib, yn, diag))]
     for copy in stat_copies:
@@ -74,7 +74,7 @@
     def d2d_copy(t, r):
         plane = (1 - y) if t == 0 else y
         start = pl.multiple_of((1 - c) * 2 * own_rows + plane * own_rows + r * rows, rows)
-        return remote(acc_ref.at[pl.ds(start, rows), :], d2d_in.at[t, r], dd_s.at[2 * r + t], dd_r.at[2 * r + t], sp=sib)
+        return remote(acc_ref.at[pl.ds(start, rows), :], d2d_in.at[t, r], dd_s, dd_r.at[2 * r + t], sp=sib)
 
     d2d_copies = [[d2d_copy(t, r) for r in range(HALVES)] for t in range(2)]
     for t in range(2):
@@ -82,7 +82,7 @@
             d2d_copies[t][r].start()
 
     lanes = pl.ds(pl.multiple_of(c * 2 * own_rows, 128), 2 * own_rows)
-    stat_copies[0].wait()
+    stat_copies[0].wait_recv()
     peaks = [stats_ref[0:heads, lanes], stat_in[0, 0:heads, :]]
     sums = [stats_ref[heads:2 * heads, lanes], stat_in[0, heads:2 * heads, :]]
     chip_top = jnp.maximum(peaks[0], peaks[1])
@@ -98,17 +98,17 @@
         return mine + d2d_in[t, r, :, cols] * fac_ref[0, pl.ds(base, rows), heads + j:heads + j + 1]
 
     def y_copy(r):
-        return remote(y_out.at[r], y_in.at[r], yy_s.at[r], yy_r.at[r], sp=yn)
+        return remote(y_out.at[r], y_in.at[r], yy_s, yy_r.at[r], sp=yn)
 
     y_copies = [y_copy(r) for r in range(HALVES)]
     for r in range(HALVES):
-        d2d_copies[0][r].wait()
+        d2d_copies[0][r].wait_recv()
         for j in range(heads):
             y_out[r, :, j * 128:(j + 1) * 128] = combined(0, r, j)
         y_copies[r].start()
 
     for copy in stat_copies[1:]:
-        copy.wait()
+        copy.wait_recv()
     peaks += [stat_in[i, 0:heads, :] for i in (1, 2)]
     sums += [stat_in[i, heads:2 * heads, :] for i in (1, 2)]
     far_top = jnp.maximum(peaks[2], peaks[3])
@@ -136,8 +136,8 @@
         return remote(fall.at[owner, k], fall.at[owner, k], gs_s, gs_r.at[k], sp=sib)
 
     def merge(r):
-        d2d_copies[1][r].wait()
-        y_copies[r].wait()
+        d2d_copies[1][r].wait_recv()
+        y_copies[r].wait_recv()
         base = pl.multiple_of(y * own_rows + r * rows, rows)
         for j in range(heads):
             near = combined(1, r, j) * fac_ref[1, pl.ds(base, rows), j:j + 1]
@@ -221,6 +221,9 @@
     def _():
         all_sent(pbuf, p_s, tp=inner_z)
 
+    all_sent(stat_in, st_s, sp=sib)
+    all_sent(d2d_in, dd_s, sp=sib)
+    all_sent(y_out, yy_s, sp=yn)
     all_sent(fall.at[sp], fy_s, sp=yn)
     all_sent(fall.at[sp], fs_s, sp=sib)
     all_sent(fall.at[yn], gs_s, sp=sib)
@@ -253,7 +256,7 @@
             f32(chunks, rows, COLS),
             f32(chunks, rows, COLS),
             f32(4, chunks, rows, COLS),
-            pltpu.SemaphoreType.DMA, pltpu.SemaphoreType.DMA, dma(3), dma(3), dma(2 * HALVES), dma(2 * HALVES), dma(HALVES), dma(HALVES),
+            pltpu.SemaphoreType.DMA, pltpu.SemaphoreType.DMA, pltpu.SemaphoreType.DMA, dma(3), pltpu.SemaphoreType.DMA, dma(2 * HALVES), pltpu.SemaphoreType.DMA, dma(HALVES),
         ] + [pltpu.SemaphoreType.DMA, dma(chunks)] * 6,
         compiler_params=pltpu.CompilerParams(collective_id=0, has_side_effects=True, vmem_limit_bytes=int(COMBINE_VMEM * 2**20)),
         name='combine',

time: 62.7 us -> 62.5 us (level)
  no operation moved by 1% of the time
where the time goes in v8:
time: 62.5 us; the launch traced here: 62.4 us
  Pallas kernels  60.4 us (97%)
  local copies, waits for them, and re-layouts  1.32 us (2%)
  between operations  0.65 us (1%)
    pallas_call x1, Pallas kernels, combine(): pl.pallas_call(combine_kernel, out_shape=jax.ShapeDtypeStruct((batch, fea...  47.2 us
    pallas_call x1, Pallas kernels, attend(): pl.pallas_call(attend_kernel, out_shape=[cache, cache, jax.ShapeDtypeStru...  13.2 us
    unnamed x1, local copies, waits for them, and re-layouts  1.32 us

profile of v8, /device:TPU:0, one launch (start us, length us, event | category | flops | bytes accessed | tf_op | source)
XLA Modules:
  0.0 62.4 jit_solution(1469832479951355258)
XLA Ops:
  0.6 13.2 %attend.1 = (bf16[16384,128]{1,0:T(8,128)(2,1)}, bf16[16384,128]{1,0:T(8,128)(2,1)}, f32[256,1024]{1,0:T(8,128)S(1)}, f32[16,256]{1,0:T(8,128)S(1)}) custom-call(s32[256]{0:T(256)} %len_hbm.1, bf16[256,4096]{1,0:T(8,128)(2,1)} %hid_hbm.3, bf16[4096]{0:T(1024)(128)(2,1)} %gain_hbm.1, bf16[4096,1024]{1,0:T(8,128)(2,1)} %wq_hbm.1, bf16[4096,256]{1,0:T(8,128)(2,1)} %wk_hbm.1, ...), custom_call_target="tpu_custom_call" | custom-call | tf_op jit(solution)/shard_map/attend/pallas_call | solution.py:431
  13.8 47.2 %combine.1 = bf16[256,4096]{1,0:T(8,128)(2,1)S(1)} custom-call(f32[256,1024]{1,0:T(8,128)S(1)} %get-tuple-element.7.acc_ref, f32[16,256]{1,0:T(8,128)S(1)} %get-tuple-element.8.stats_ref, bf16[256,4096]{1,0:T(8,128)(2,1)} %hid_hbm.3, bf16[1024,4096]{1,0:T(8,128)(2,1)} %w_hbm.1), custom_call_target="tpu_custom_call" | custom-call | tf_op jit(solution)/shard_map/combine/pallas_call | solution.py:240
  61.1 1.3 %copy.13 = bf16[256,4096]{1,0:T(8,128)(2,1)} copy(bf16[256,4096]{1,0:T(8,128)(2,1)S(1)} %combine.1) | data formatting | bytes 4194304
